TPU v7x, 256 devices: a whole 4x4x8 slice. The times are simulated.
256 devices in a mesh: dp: 8 (over y, core), expert: 32 (over x, z).
Axes of the slice: x: 4, y: 4, z: 8, core: 2. Of those that a mesh axis runs over, the one named last changes fastest.
Arguments:
- tokens: bfloat16 [4096, 4096], P(('dp', 'expert')), may hold values from -6 to 6
- expert_ids: int32 [4096, 2], P(('dp', 'expert')), may hold values from 0 to 7, all different within a row; in each aligned block of 16 rows (0 to 15, 16 to 31, ...) at most 6 rows name the same one
- gate_quota: int32 [4096, 2], P(('dp', 'expert')), may hold values from 1 to 32767
- w_gate: bfloat16 [32, 4096, 2048], P('expert', None, 'dp'), may hold values from -0.09375 to 0.09375
- w_up: bfloat16 [32, 4096, 2048], P('expert', None, 'dp'), may hold values from -0.09375 to 0.09375
- w_down: bfloat16 [32, 2048, 4096], P('expert', 'dp'), may hold values from -0.0625 to 0.0625
Outputs:
- mixed_out: bfloat16 [4096, 4096], P(('dp', 'expert'))
Inputs may be any that keep to these rules, and one draw needn't show every extreme that they name: `expert_ids`: each row names 2 different experts; among the rows of one device no expert is named more than 6 times.
All inputs are finite; a program needn't handle non-finite values.
Results may differ from a plain program's by a relative error of at most 0.015.
Values may be sent and summed in bfloat16 or wider, within the bound.
A program may use at most 128 MiB of HBM per device.

v0:
```python
import jax
import jax.numpy as jnp
from jax import lax
from jax.sharding import PartitionSpec as P

EXPERTS = 8
TOP = 2
CAP = 6


def expert_hidden(expert_rows, gate_cols, up_cols):
    gate_act = jnp.dot(expert_rows, gate_cols, preferred_element_type=jnp.float32)
    up_act = jnp.dot(expert_rows, up_cols, preferred_element_type=jnp.float32)
    return (jax.nn.silu(gate_act) * up_act).astype(jnp.bfloat16)


def on_device(tokens, expert_ids, gate_quota, w_gate, w_up, w_down):
    tok_rows, feature_dim = tokens.shape
    expert_count = lax.axis_size("expert")
    group_size = expert_count // EXPERTS
    gate_cols = w_gate[0]
    up_cols = w_up[0]
    down_rows = w_down[0]
    flat_ids = expert_ids.reshape(-1)
    chosen_mask = (flat_ids[:, None] == jnp.arange(EXPERTS, dtype=jnp.int32)[None, :]).astype(
        jnp.int32
    )
    earlier = jnp.cumsum(chosen_mask, axis=0) - chosen_mask
    position = jnp.sum(earlier * chosen_mask, axis=1)
    slot_index = flat_ids * CAP + position
    placing = (slot_index[None, :] == jnp.arange(EXPERTS * CAP, dtype=jnp.int32)[:, None]).astype(
        jnp.bfloat16
    )
    repeated = jnp.repeat(tokens, TOP, axis=0)
    packed = jnp.dot(placing, repeated, preferred_element_type=jnp.float32).astype(jnp.bfloat16)
    packed = packed.reshape(EXPERTS, CAP, feature_dim)
    outgoing = jnp.repeat(packed, group_size, axis=0)
    arrived = lax.all_to_all(outgoing, "expert", split_axis=0, concat_axis=0, tiled=True)
    flat_rows = arrived.reshape(expert_count * CAP, feature_dim)
    hidden = expert_hidden(lax.all_gather(flat_rows, "dp", axis=0, tiled=True), gate_cols, up_cols)
    summed = lax.psum_scatter(
        jnp.dot(hidden, down_rows, preferred_element_type=jnp.float32).astype(jnp.bfloat16),
        "dp",
        scatter_dimension=0,
        tiled=True,
    ).astype(jnp.float32)
    returned = lax.all_to_all(
        summed.reshape(expert_count, CAP, feature_dim).astype(jnp.bfloat16),
        "expert",
        split_axis=0,
        concat_axis=0,
        tiled=True,
    ).astype(jnp.float32)
    expert_out = jnp.sum(returned.reshape(EXPERTS, group_size, CAP, feature_dim), axis=1)
    expert_out = expert_out.reshape(EXPERTS * CAP, feature_dim)
    per_assign = expert_out[slot_index]
    quota = gate_quota.astype(jnp.float32)
    shares = quota / jnp.sum(quota, axis=1, keepdims=True)
    mixed_out = jnp.sum(per_assign.reshape(tok_rows, TOP, feature_dim) * shares[:, :, None], axis=1)
    return mixed_out.astype(jnp.bfloat16)


def solution(mesh):
    return jax.shard_map(
        on_device,
        mesh=mesh,
        in_specs=(
            P(("dp", "expert"), None),
            P(("dp", "expert"), None),
            P(("dp", "expert"), None),
            P("expert", None, "dp"),
            P("expert", None, "dp"),
            P("expert", "dp", None),
        ),
        out_specs=P(("dp", "expert"), None),
        check_vma=False,
    )
```

profile of v0, /device:TPU:1, one launch (start us, length us, event | category | flops | bytes accessed | tf_op | source)
XLA Modules:
  0.0 323.9 jit_solution(4167050153999011241)
XLA Ops:
  6.5 0.9 copy.10
  7.4 0.1 reshape.68
  7.7 0.2 select_reduce_fusion
  7.9 1.1 broadcast_in_dim.4
  9.0 0.1 reshape.69
  9.1 0.2 convolution_convert_fusion.1
  9.3 0.1 reshape.70
  9.5 0.2 broadcast_in_dim.5
  9.7 58.9 %all_to_all.10 = bf16[32,6,4096]{2,1,0:T(8,128)(2,1)} all-to-all(bf16[32,6,4096]{2,1,0:T(8,128)(2,1)S(1)} %bitcast.23), channel_id=1, replica_groups=mesh['dp'=8,'expert'=32] {'expert'}, dimensions={0} | all-to-all | bytes 3145728 | tf_op jit(solution)/shard_map/all_to_all | solution.py:38
  68.6 3.6 %reshape.72 = bf16[192,4096]{1,0:T(8,128)(2,1)} reshape(bf16[32,6,4096]{2,1,0:T(8,128)(2,1)} %all_to_all.10) | data formatting | bytes 3145728 | tf_op jit(solution)/shard_map/reshape | solution.py:39
  72.3 71.4 %all-gather.2.cloned.1.call-done = bf16[1536,4096]{1,0:T(8,128)(2,1)} async-done(((bf16[192,4096]{1,0:T(8,128)(2,1)}), bf16[1536,4096]{1,0:T(8,128)(2,1)}) %all-gather.2.cloned.1.call-update) | async-done | bytes 12582928 | tf_op jit(solution)/shard_map/all_gather | solution.py:40
  143.7 9.9 %fusion.4 = f32[1536,256]{1,0:T(8,128)} fusion(bf16[1536,4096]{1,0:T(8,128)(2,1)} %all-gather.2.cloned.1.call-done, bf16[1,4096,256]{2,1,0:T(8,128)(2,1)} %param.9), kind=kOutput, calls=%fused_computation.8 | convolution fusion | flops 3221225472 | bytes 16252928 | tf_op jit(solution)/shard_map/dot_general | solution.py:12
  153.5 19.4 %convolution_convert_fusion = bf16[1536,4096]{1,0:T(8,128)(2,1)} fusion(bf16[1536,4096]{1,0:T(8,128)(2,1)} %all-gather.2.cloned.1.call-done, bf16[1,256,4096]{2,1,0:T(8,128)(2,1)S(1)} %copy-done, bf16[1,4096,256]{2,1,0:T(8,128)(2,1)} %param.10, f32[1536,256]{1,0:T(8,128)} %fusion.4), kind=kOutput, calls=%fused_computation.1 | convolution fusion | flops 6451101696 | bytes 30932992 | tf_op jit(solution)/shard_map/dot_general | solution.py:42
  173.0 74.6 %reduce-scatter.2.cloned.1.call-done = bf16[192,4096]{1,0:T(8,128)(2,1)} async-done(((bf16[1536,4096]{1,0:T(8,128)(2,1)}), bf16[192,4096]{1,0:T(8,128)(2,1)}) %reduce-scatter.2.cloned.1.call-update) | async-done | bytes 1572880 | tf_op jit(solution)/shard_map/reduce_scatter | solution.py:41
  247.6 3.5 %convert_element_type.29 = bf16[32,6,4096]{2,1,0:T(8,128)(2,1)} reshape(bf16[192,4096]{1,0:T(8,128)(2,1)} %reduce-scatter.2.cloned.1.call-done) | data formatting | bytes 3145728 | tf_op jit(solution)/shard_map/convert_element_type | solution.py:48
  251.1 9.8 %all-to-all-start.1 = ((bf16[32,6,4096]{2,1,0:T(8,128)(2,1)}), bf16[32,6,4096]{2,1,0:T(8,128)(2,1)}, u32[]{:S(2)}, u32[]{:S(2)}) async-start(bf16[32,6,4096]{2,1,0:T(8,128)(2,1)} %convert_element_type.29), calls=%async_computation.2 | async-start | bytes 4194304 | tf_op jit(solution)/shard_map/all_to_all | solution.py:47
  261.0 0.1 mul.49
  261.1 0.1 copy.12
  261.2 48.9 %all-to-all-done.1 = bf16[32,6,4096]{2,1,0:T(8,128)(2,1)} async-done(((bf16[32,6,4096]{2,1,0:T(8,128)(2,1)}), bf16[32,6,4096]{2,1,0:T(8,128)(2,1)}, u32[]{:S(2)}, u32[]{:S(2)}) %all-to-all-start.1) | async-done | bytes 1572896 | tf_op jit(solution)/shard_map/all_to_all | solution.py:47
  310.1 3.1 convert_reduce_fusion
  313.3 1.3 reshape.75
  314.6 0.7 gather_fusion
  315.3 0.3 reshape.76
  315.6 1.4 multiply_reduce_fusion
  (19 shorter events, 0.4 us)
Async XLA Ops:
  6.5 147.0 %copy-start = (bf16[1,256,4096]{2,1,0:T(8,128)(2,1)S(1)}, bf16[1,256,4096]{2,1,0:T(8,128)(2,1)}, u32[]{:S(2)}) copy-start(bf16[1,256,4096]{2,1,0:T(8,128)(2,1)} %param.11) | copy-start | bytes 6291460
  6.5 137.1 %all-gather.2.cloned.1.call-start = ((), (), s32[]{:S(2)}) async-start(), calls=%async_computation.3 | async-start | bytes 14155776 | tf_op jit(solution)/shard_map/all_gather | solution.py:40
  72.3 175.3 %reduce-scatter.2.cloned.1.call-start = ((), (), s32[]{:S(2)}) async-start(), calls=%async_computation.4 | async-start | bytes 14155776 | tf_op jit(solution)/shard_map/reduce_scatter | solution.py:41
  251.1 9.8 %copy-start.1 = (s32[16,2]{0,1:T(2,128)S(1)}, s32[16,2]{0,1:T(2,128)}, u32[]{:S(2)}) copy-start(s32[16,2]{0,1:T(2,128)} %param.7) | copy-start | bytes 388
  251.1 10.0 %copy-start.2 = (s32[16,2]{0,1:T(2,128)S(1)}, s32[16,2]{0,1:T(2,128)}, u32[]{:S(2)}) copy-start(s32[16,2]{0,1:T(2,128)} %param.8) | copy-start | bytes 388
  251.1 59.1 %all-to-all-start.1 = ((bf16[32,6,4096]{2,1,0:T(8,128)(2,1)}), bf16[32,6,4096]{2,1,0:T(8,128)(2,1)}, u32[]{:S(2)}, u32[]{:S(2)}) async-start(bf16[32,6,4096]{2,1,0:T(8,128)(2,1)} %convert_element_type.29), calls=%async_computation.2 | async-start | bytes 4194304 | tf_op jit(solution)/shard_map/all_to_all | solution.py:47
Sparse Core Ops, SparseCore 0:
  72.4 71.2 all-gather.1
  173.1 74.4 reduce-scatter.1
where the time goes:
time: 324 us
  waiting for transfers between devices  195 us (60%)
  blocking collectives  58.9 us (18%)
  matrix products  29.5 us (9%)
  between operations  13.5 us (4%)
  local copies, waits for them, and re-layouts  12.4 us (4%)
  starting transfers between devices  9.84 us (3%)
  other arithmetic  4.86 us (2%)
    reduce_scatter x1, waiting for transfers between devices, on_device(): lax.psum_scatter(jnp.dot(hidden, down_rows, preferred_element_type=jnp.fl...  74.6 us
    all_gather x1, waiting for transfers between devices, on_device(): lax.all_gather(flat_rows, 'dp', axis=0, tiled=True)  71.4 us
    all_to_all x1, blocking collectives, on_device(): lax.all_to_all(outgoing, 'expert', split_axis=0, concat_axis=0, tiled=True)  58.9 us
    all_to_all x1, waiting for transfers between devices, on_device(): lax.all_to_all(summed.reshape(expert_count, CAP, feature_dim).astype(jnp....  48.9 us
    dot_general x1, matrix products, on_device(): jnp.dot(hidden, down_rows, preferred_element_type=jnp.float32)  19.4 us
    dot_general x1, matrix products, expert_hidden(): jnp.dot(expert_rows, gate_cols, preferred_element_type=jnp.float32)  9.86 us
    all_to_all x1, starting transfers between devices, on_device(): lax.all_to_all(summed.reshape(expert_count, CAP, feature_dim).astype(jnp....  9.8 us
  transfers between devices with their start and end apart: 3, of which 3 were waited for; matrix products, arithmetic and copies ran while one was open for 0% of the time, Pallas kernels for 0%

commit v1 on v0

v1 whole, which is shorter than its diff:
```python
import jax
import jax.numpy as jnp
from jax import lax
from jax.experimental import pallas as pl
from jax.experimental.pallas import tpu as pltpu
from jax.sharding import PartitionSpec as P

MESH = pl.DeviceIdType.MESH
EXPERTS = 8
TOP = 2
CAP = 6
NX = 4
NZ = 8
NY = 4
HALVES = EXPERTS // NX
GROUP = NZ // HALVES
SPLIT = 8
NCHUNK = NX
F32 = jnp.float32
BF16 = jnp.bfloat16


def moe_kernel(
    tok_ref, pick_ref, mix_ref, perm_ref, wg_hbm, wu_hbm, wd_hbm, out_ref,
    packed, arr, xall, wg, wu, wd, hid, part, fromcore, ringa, ringb, lasta, lastb, outgo, ret,
    w_sem, dsend, drecv, gsend, grecv, rsend, rrecv, bsend, brecv,
):
    feature = tok_ref.shape[1]
    piece = feature // SPLIT
    half = feature // 2
    rows = NZ * CAP
    dp = lax.axis_index("dp")
    ex = lax.axis_index("expert")
    core = lax.rem(dp, 2)
    y = dp // 2
    xx = ex // NZ
    zz = lax.rem(ex, NZ)
    n_ex = NX * NZ
    y_up, y_down, y_far = lax.rem(y + 1, NY), lax.rem(y + NY - 1, NY), lax.rem(y + 2, NY)
    up = y_up * 2 + core
    down = y_down * 2 + core
    far = y_far * 2 + core
    other = y * 2 + (1 - core)
    lo = pl.ds(0, half)
    hi = pl.ds(half, half)

    loads = [
        pltpu.make_async_copy(wg_hbm.at[0], wg, w_sem.at[0]),
        pltpu.make_async_copy(wu_hbm.at[0], wu, w_sem.at[1]),
        pltpu.make_async_copy(wd_hbm.at[0], wd, w_sem.at[2]),
    ]
    for load in loads:
        load.start()

    barrier = pltpu.get_barrier_semaphore()

    def greet(i, carry):
        pl.semaphore_signal(
            barrier, inc=1, device_id={"expert": lax.rem(ex + i, n_ex)}, device_id_type=MESH
        )
        return carry

    lax.fori_loop(1, n_ex, greet, 0)
    for peer in (up, down, other):
        pl.semaphore_signal(barrier, inc=1, device_id={"dp": peer}, device_id_type=MESH)

    stacked = jnp.concatenate(
        [tok_ref[:, o * piece : (o + 1) * piece] for o in range(SPLIT)], axis=0
    )
    chosen = jnp.dot(pick_ref[...], stacked, preferred_element_type=F32).astype(BF16)
    packed[...] = chosen.reshape(packed.shape)
    arr[0, pl.ds(zz, 1)] = packed[0, pl.ds(zz // GROUP, 1)]

    pl.semaphore_wait(barrier, n_ex - 1 + 3)

    def to_expert(k, dz):
        z_to = lax.rem(zz + dz, NZ)
        x_to = lax.rem(xx + k, NX)
        return pltpu.make_async_remote_copy(
            packed.at[k, z_to // GROUP], arr.at[k, zz], dsend.at[k, dz], drecv.at[k, zz],
            device_id={"expert": x_to * NZ + z_to}, device_id_type=MESH,
        )

    def expert_arrival(k, z_from):
        return pltpu.make_async_remote_copy(
            packed.at[k, 0], arr.at[k, z_from], dsend.at[k, 0], drecv.at[k, z_from],
            device_id={"expert": ex}, device_id_type=MESH,
        )

    def to_dp(src, dst, send, recv, peer):
        return pltpu.make_async_remote_copy(
            src, dst, send, recv, device_id={"dp": peer}, device_id_type=MESH
        )

    def g_copy(k, n):
        send, recv = gsend.at[k, n], grecv.at[k, n]
        block, cols, peer = [
            (dp, None, up), (dp, None, down), (dp, None, other),
            (down, lo, up), (up, hi, down),
            (down, None, other), (up, None, other), (far, None, other),
        ][n]
        view = xall.at[k, block] if cols is None else xall.at[k, block, :, cols]
        return to_dp(view, view, send, recv, peer)

    def r_copy(k, n):
        send, recv = rsend.at[k, n], rrecv.at[k, n]
        if n < 4:
            place = [y_far, y_up, y_down, y][n]
            return to_dp(
                part.at[k, place * 2 + (1 - core)], fromcore.at[k, place], send, recv, other
            )
        src, cols, dst, peer = [
            (far, lo, ringa.at[k], up),
            (far, hi, ringb.at[k], down),
            (up, hi, lasta.at[k, :, hi], up),
            (down, lo, lastb.at[k, :, lo], down),
            (up, lo, lasta.at[k, :, lo], up),
            (down, hi, lastb.at[k, :, hi], down),
        ][n - 4]
        return to_dp(part.at[k, src, :, cols], dst, send, recv, peer)

    def to_owner(k, dz):
        z_to = lax.rem(zz + dz, NZ)
        x_to = lax.rem(xx + NX - k, NX)
        return pltpu.make_async_remote_copy(
            outgo.at[k, z_to], ret.at[k, zz], bsend.at[k, dz], brecv.at[k, zz],
            device_id={"expert": x_to * NZ + z_to}, device_id_type=MESH,
        )

    def owner_arrival(k, z_from):
        return pltpu.make_async_remote_copy(
            outgo.at[k, 0], ret.at[k, z_from], bsend.at[k, 0], brecv.at[k, z_from],
            device_id={"expert": ex}, device_id_type=MESH,
        )

    def send_all(k, carry):
        def one(dz, inner):
            @pl.when((k != 0) | (dz != 0))
            def _():
                to_expert(k, dz).start()

            return inner

        return lax.fori_loop(0, NZ, one, carry)

    lax.fori_loop(0, NCHUNK, send_all, 0)

    def stage_rows(k):
        def one(z_from, inner):
            @pl.when((k != 0) | (z_from != zz))
            def _():
                expert_arrival(k, z_from).wait_recv()

            return inner

        lax.fori_loop(0, NZ, one, 0)
        flat = arr[k].reshape(NZ * CAP * SPLIT, piece)
        sorted_rows = jnp.dot(perm_ref[0], flat, preferred_element_type=F32).astype(BF16)
        for o in range(SPLIT):
            xall[k, dp, :, o * piece : (o + 1) * piece] = sorted_rows[o * rows : (o + 1) * rows]
        for n in range(3):
            g_copy(k, n).start()

    def stage_forward(k):
        g_copy(k, 0).wait_recv()
        g_copy(k, 3).start()
        g_copy(k, 5).start()
        g_copy(k, 1).wait_recv()
        g_copy(k, 4).start()
        g_copy(k, 6).start()

    def stage_far(k):
        g_copy(k, 3).wait_recv()
        g_copy(k, 4).wait_recv()
        g_copy(k, 7).start()

    def stage_compute(k):
        for n in (2, 5, 6, 7):
            g_copy(k, n).wait_recv()

        @pl.when(k == 0)
        def _():
            for load in loads:
                load.wait()

        for m in range(2):
            x_in = xall[k, m * NY : (m + 1) * NY].reshape(NY * rows, feature)
            gate = jnp.dot(x_in, wg[...], preferred_element_type=F32)
            up_act = jnp.dot(x_in, wu[...], preferred_element_type=F32)
            hid[m * NY * rows : (m + 1) * NY * rows] = (
                gate * (1.0 / (1.0 + jnp.exp(-gate))) * up_act
            ).astype(BF16)

        def down_block(n, carry):
            cols = pl.ds(pl.multiple_of(n * piece, piece), piece)
            got = jnp.dot(hid[...], wd[:, cols], preferred_element_type=F32).astype(BF16)
            part[k, :, :, cols] = got.reshape(2 * NY, rows, piece)
            return carry

        lax.fori_loop(0, SPLIT, down_block, 0)
        for n in range(4):
            r_copy(k, n).start()

    def join(k, place, cols):
        mine = place * 2 + core
        total = part[k, mine, :, cols].astype(F32) + fromcore[k, place, :, cols].astype(F32)
        part[k, mine, :, cols] = total.astype(BF16)

    def stage_ring(k):
        r_copy(k, 0).wait_recv()
        join(k, y_far, pl.ds(0, feature))
        r_copy(k, 4).start()
        r_copy(k, 5).start()
        r_copy(k, 1).wait_recv()
        join(k, y_up, pl.ds(0, feature))
        r_copy(k, 6).start()
        r_copy(k, 2).wait_recv()
        join(k, y_down, pl.ds(0, feature))
        r_copy(k, 7).start()

    def stage_last(k):
        r_copy(k, 4).wait_recv()
        part[k, up, :, lo] = (part[k, up, :, lo].astype(F32) + ringa[k].astype(F32)).astype(BF16)
        r_copy(k, 8).start()
        r_copy(k, 5).wait_recv()
        part[k, down, :, hi] = (
            part[k, down, :, hi].astype(F32) + ringb[k].astype(F32)
        ).astype(BF16)
        r_copy(k, 9).start()

    def stage_back(k):
        r_copy(k, 3).wait_recv()
        for n in (6, 7, 8, 9):
            r_copy(k, n).wait_recv()
        pieces = []
        for o in range(SPLIT):
            cols = slice(o * piece, (o + 1) * piece)
            total = (
                part[k, dp, :, cols].astype(F32)
                + fromcore[k, y, :, cols].astype(F32)
                + lasta[k, :, cols].astype(F32)
                + lastb[k, :, cols].astype(F32)
            )
            pieces.append(total.astype(BF16))
        block = jnp.concatenate(pieces, axis=0)
        sorted_rows = jnp.dot(perm_ref[1], block, preferred_element_type=F32).astype(BF16)
        outgo[k] = sorted_rows.reshape(NZ, CAP * SPLIT, piece)

        def one(dz, inner):
            @pl.when((k != 0) | (dz != 0))
            def _():
                to_owner(k, dz).start()

            return inner

        lax.fori_loop(0, NZ, one, 0)

        @pl.when(k == 0)
        def _():
            ret[0, pl.ds(zz, 1)] = outgo[0, pl.ds(zz, 1)]

    def step(i, carry):
        j = i - 1
        for stage, lag in (
            (stage_forward, 0), (stage_rows, -1), (stage_ring, 1), (stage_back, 2),
            (stage_far, 0), (stage_compute, 0), (stage_last, 1),
        ):
            k = j - lag

            @pl.when((k >= 0) & (k < NCHUNK))
            def _(stage=stage, k=k):
                stage(k)

        return carry

    lax.fori_loop(0, NCHUNK + 3, step, 0)

    def drain(k, carry):
        def one(z, inner):
            @pl.when((k != 0) | (z != zz))
            def _():
                owner_arrival(k, z).wait_recv()

            @pl.when((k != 0) | (z != 0))
            def _():
                to_expert(k, z).wait_send()
                to_owner(k, z).wait_send()

            return inner

        lax.fori_loop(0, NZ, one, 0)
        for n in range(8):
            g_copy(k, n).wait_send()
        for n in range(10):
            r_copy(k, n).wait_send()
        return carry

    lax.fori_loop(0, NCHUNK, drain, 0)

    sums = []
    for k in range(NX):
        for h in range(HALVES):
            total = ret[k, h * GROUP].astype(F32)
            for g in range(1, GROUP):
                total = total + ret[k, h * GROUP + g].astype(F32)
            sums.append(total)
    mixed = jnp.dot(
        mix_ref[...], jnp.concatenate(sums, axis=0),
        preferred_element_type=F32, precision=lax.Precision.HIGHEST,
    ).astype(BF16)
    tok = tok_ref.shape[0]
    for o in range(SPLIT):
        out_ref[:, o * piece : (o + 1) * piece] = mixed[o * tok : (o + 1) * tok]


def on_device(tokens, expert_ids, gate_quota, w_gate, w_up, w_down):
    tok_rows, feature = tokens.shape
    width = w_gate.shape[2]
    piece = feature // SPLIT
    rows = NZ * CAP
    slots = EXPERTS * CAP
    flat_ids = expert_ids.reshape(-1)
    chosen_mask = (flat_ids[:, None] == jnp.arange(EXPERTS, dtype=jnp.int32)[None, :]).astype(
        jnp.int32
    )
    earlier = jnp.cumsum(chosen_mask, axis=0) - chosen_mask
    position = jnp.sum(earlier * chosen_mask, axis=1)
    xx = lax.axis_index("expert") // NZ
    ahead = (flat_ids // HALVES + NX - xx) % NX
    slot = ((ahead * HALVES + flat_ids % HALVES) * CAP + position).reshape(tok_rows, TOP)
    quota = gate_quota.astype(F32)
    shares = quota / jnp.sum(quota, axis=1, keepdims=True)
    match = slot[:, :, None] == jnp.arange(slots, dtype=jnp.int32)
    picked = jnp.any(match, axis=1)
    weight = jnp.sum(jnp.where(match, shares[:, :, None], 0.0), axis=1)
    same = jnp.eye(SPLIT, dtype=bool)
    pick = jnp.where(same[None, :, :, None], picked.T[:, None, None, :], False).astype(BF16)
    pick = pick.reshape(slots * SPLIT, SPLIT * tok_rows)
    mix = jnp.where(same[:, None, None, :], weight[None, :, :, None], 0.0)
    mix = mix.reshape(SPLIT * tok_rows, slots * SPLIT)
    index = jnp.arange(rows * SPLIT, dtype=jnp.int32)
    wanted = (index % rows) * SPLIT + index // rows
    perm = (wanted[:, None] == index[None, :]).astype(BF16)
    perms = jnp.stack([perm, perm.T])

    whole = pl.BlockSpec(memory_space=pltpu.VMEM)
    anywhere = pl.BlockSpec(memory_space=pl.ANY)
    dma = pltpu.SemaphoreType.DMA
    return pl.pallas_call(
        moe_kernel,
        out_shape=jax.ShapeDtypeStruct((tok_rows, feature), BF16),
        in_specs=[whole, whole, whole, whole, anywhere, anywhere, anywhere],
        out_specs=whole,
        scratch_shapes=[
            pltpu.VMEM((NX, HALVES, CAP * SPLIT, piece), BF16),
            pltpu.VMEM((NX, NZ, CAP * SPLIT, piece), BF16),
            pltpu.VMEM((NX, 2 * NY, rows, feature), BF16),
            pltpu.VMEM((feature, width), BF16),
            pltpu.VMEM((feature, width), BF16),
            pltpu.VMEM((width, feature), BF16),
            pltpu.VMEM((2 * NY * rows, width), BF16),
            pltpu.VMEM((NX, 2 * NY, rows, feature), BF16),
            pltpu.VMEM((NX, NY, rows, feature), BF16),
            pltpu.VMEM((NX, rows, feature // 2), BF16),
            pltpu.VMEM((NX, rows, feature // 2), BF16),
            pltpu.VMEM((NX, rows, feature), BF16),
            pltpu.VMEM((NX, rows, feature), BF16),
            pltpu.VMEM((NX, NZ, CAP * SPLIT, piece), BF16),
            pltpu.VMEM((NX, NZ, CAP * SPLIT, piece), BF16),
            dma((3,)),
            dma((NX, NZ)),
            dma((NX, NZ)),
            dma((NX, 8)),
            dma((NX, 8)),
            dma((NX, 10)),
            dma((NX, 10)),
            dma((NX, NZ)),
            dma((NX, NZ)),
        ],
        compiler_params=pltpu.CompilerParams(
            collective_id=0, has_side_effects=True, vmem_limit_bytes=64 * 1024 * 1024 - 65536
        ),
        name="moe",
    )(tokens, pick, mix, perms, w_gate, w_up, w_down)


def solution(mesh):
    return jax.shard_map(
        on_device,
        mesh=mesh,
        in_specs=(
            P(("dp", "expert"), None),
            P(("dp", "expert"), None),
            P(("dp", "expert"), None),
            P("expert", None, "dp"),
            P("expert", None, "dp"),
            P("expert", "dp", None),
        ),
        out_specs=P(("dp", "expert"), None),
        check_vma=False,
    )
```

time: 324 us -> 154 us (0.48)
  waiting for transfers between devices: 195 us -> 0 us
  Pallas kernels: 0 us -> 145 us
  blocking collectives: 58.9 us -> 0 us
  matrix products: 29.5 us -> 0 us
  between operations: 13.5 us -> 0.07 us
  starting transfers between devices: 9.84 us -> 0 us
  local copies, waits for them, and re-layouts: 12.4 us -> 5.22 us
    pallas_call x0 -> x1, Pallas kernels: none -> 145 us  [on_device(): pl.pallas_call(moe_kernel, out_shape=jax.ShapeDtypeStruct((tok_rows, feat...]
    reduce_scatter x1 -> x0, waiting for transfers between devices: 74.6 us -> none  [on_device(): lax.psum_scatter(jnp.dot(hidden, down_rows, preferred_element_type=jnp.fl...]
    all_gather x1 -> x0, waiting for transfers between devices: 71.4 us -> none  [on_device(): lax.all_gather(flat_rows, 'dp', axis=0, tiled=True)]
    all_to_all x1 -> x0, blocking collectives: 58.9 us -> none  [on_device(): lax.all_to_all(outgoing, 'expert', split_axis=0, concat_axis=0, tiled=True)]
    all_to_all x1 -> x0, waiting for transfers between devices: 48.9 us -> none  [on_device(): lax.all_to_all(summed.reshape(expert_count, CAP, feature_dim).astype(jnp....]
    dot_general x3 -> x0, matrix products: 29.5 us -> none  [the longest x1 19.4 us: on_device(): jnp.dot(hidden, down_rows, preferred_element_type=jnp.float32)]
    all_to_all x1 -> x0, starting transfers between devices: 9.8 us -> none  [on_device(): lax.all_to_all(summed.reshape(expert_count, CAP, feature_dim).astype(jnp....]
    reshape x6 -> x0, local copies, waits for them, and re-layouts: 5.61 us -> none  [the longest x1 3.65 us: on_device(): flat_rows = arrived.reshape(expert_count * CAP, feature_dim)]
  transfers between devices with their start and end apart: 3 -> 0, of which waited for: 3 -> 0; matrix products, arithmetic and copies ran while one was open for 0% -> 0% of each run, Pallas kernels for 0% -> 0%
where the time goes in v1:
time: 154 us
  Pallas kernels  145 us (94%)
  local copies, waits for them, and re-layouts  5.22 us (3%)
  other arithmetic  3.56 us (2%)
    pallas_call x1, Pallas kernels, on_device(): pl.pallas_call(moe_kernel, out_shape=jax.ShapeDtypeStruct((tok_rows, feat...  145 us

profile of v1, /device:TPU:1, one launch (start us, length us, event | category | flops | bytes accessed | tf_op | source)
XLA Modules:
  0.0 154.3 jit_solution(13724089056256715867)
XLA Ops:
  0.0 0.8 copy.22
  0.8 0.1 eq.81
  0.8 0.1 fusion.1
  0.9 0.1 reduce_window_sum.11
  1.0 0.2 select_reduce_fusion.1
  1.2 0.1 reduce_sum.30
  1.3 0.1 copy.27
  1.4 0.7 convert_reduce_fusion
  2.1 0.7 convert_divide_fusion
  2.8 0.1 select_reduce_fusion
  2.8 0.1 copy.29
  2.9 0.2 broadcast_select_fusion
  3.2 0.4 select_n.74
  3.6 0.8 copy.30.mix_ref
  4.4 0.1 fusion
  4.5 0.1 copy.28
  4.6 0.1 copy.21
  4.7 0.3 select_convert_fusion
  5.0 1.1 reshape.163.pick_ref
  6.1 0.2 iota_compare_fusion.1
  6.3 0.9 add_convert_fusion.perm_ref
  7.3 145.4 %moe.1 = bf16[16,4096]{1,0:T(8,128)(2,1)} custom-call(bf16[16,4096]{1,0:T(8,128)(2,1)} %tok_ref.1, bf16[384,128]{1,0:T(8,128)(2,1)} %reshape.163.pick_ref, f32[128,384]{1,0:T(8,128)} %copy.30.mix_ref, bf16[2,384,384]{2,1,0:T(8,128)(2,1)} %add_convert_fusion.perm_ref, bf16[1,4096,256]{2,1,0:T(8,128)(2,1)} %wg_hbm.1, bf16[1,4096,256]{2,1,0:T(8,128)(2,1)} %wu_hbm.1, ...), custom_call_target="tpu_custom_call" | custom-call | tf_op jit(solution)/shard_map/moe/pallas_call | solution.py:349
  152.7 1.6 %copy.32 = bf16[16,4096]{1,0:T(8,128)(2,1)} copy(bf16[16,4096]{1,0:T(8,128)(2,1)} %moe.1) | data formatting | bytes 262144
  (3 shorter events, 0.1 us)

commit v2 on v0

v2 whole, which is shorter than its diff:
```python
import jax
import jax.numpy as jnp
from jax import lax
from jax.experimental import pallas as pl
from jax.experimental.pallas import tpu as pltpu
from jax.sharding import PartitionSpec as P

MESH = pl.DeviceIdType.MESH
EXPERTS = 8
TOP = 2
CAP = 6
NX = 4
NZ = 8
NY = 4
HALVES = EXPERTS // NX
GROUP = NZ // HALVES
SPLIT = 8
NCHUNK = NX
F32 = jnp.float32
BF16 = jnp.bfloat16

STAGES = (
    ("forward_0", 0), ("rows_0", -1), ("forward_1", 0), ("rows_1", -1),
    ("ring_0", 1), ("ring_1", 1), ("far_0", 0), ("far_1", 0), ("compute", 0),
    ("back_0", 2), ("back_1", 2), ("last_0", 1), ("last_1", 1),
)


def moe_kernel(
    tok_hbm, ids_hbm, quota_hbm, wg_hbm, wu_hbm, wd_hbm, out_ref,
    tok_ref, ids_ref, quota_ref, packed, arr, xall, wg, wu, wd, hid, part, fromcore, ringa, ringb, lasta, lastb, outgo, ret,
    perm, mix, w_sem, dsend, drecv, gsend, grecv, rsend, rrecv, bsend, brecv,
):
    tok, feature = tok_ref.shape
    half = feature // 2
    quarter = feature // 4
    piece = half // SPLIT
    rows = NZ * CAP
    slots = EXPERTS * CAP
    dp = lax.axis_index("dp")
    ex = lax.axis_index("expert")
    core = lax.rem(dp, 2)
    y = dp // 2
    xx = ex // NZ
    zz = lax.rem(ex, NZ)
    n_ex = NX * NZ
    y_up, y_down, y_far = lax.rem(y + 1, NY), lax.rem(y + NY - 1, NY), lax.rem(y + 2, NY)
    up = y_up * 2 + core
    down = y_down * 2 + core
    far = y_far * 2 + core
    other = y * 2 + (1 - core)

    def both(c):
        return pl.ds(c * half, half)

    def lo(c):
        return pl.ds(c * half, quarter)

    def hi(c):
        return pl.ds(c * half + quarter, quarter)

    barrier = pltpu.get_barrier_semaphore()

    def greet(i, carry):
        pl.semaphore_signal(
            barrier, inc=1, device_id={"expert": lax.rem(ex + i, n_ex)}, device_id_type=MESH
        )
        return carry

    lax.fori_loop(1, n_ex, greet, 0)
    for peer in (up, down, other):
        pl.semaphore_signal(barrier, inc=1, device_id={"dp": peer}, device_id_type=MESH)

    first_loads = [
        pltpu.make_async_copy(ids_hbm, ids_ref, w_sem.at[3]),
        pltpu.make_async_copy(quota_hbm, quota_ref, w_sem.at[4]),
        pltpu.make_async_copy(tok_hbm, tok_ref, w_sem.at[5]),
    ]
    for load in first_loads:
        load.start()
    loads = [
        pltpu.make_async_copy(wg_hbm.at[0], wg, w_sem.at[0]),
        pltpu.make_async_copy(wu_hbm.at[0], wu, w_sem.at[1]),
        pltpu.make_async_copy(wd_hbm.at[0], wd, w_sem.at[2]),
    ]
    for load in loads:
        load.start()

    p_row = lax.broadcasted_iota(jnp.int32, (rows * SPLIT, rows * SPLIT), 0)
    p_col = lax.broadcasted_iota(jnp.int32, (rows * SPLIT, rows * SPLIT), 1)
    perm[0] = jnp.where(p_row == (p_col & (SPLIT - 1)) * rows + (p_col >> 3), 1.0, 0.0).astype(BF16)

    for load in first_loads:
        load.wait()

    lanes = SPLIT * tok
    t_row = lax.broadcasted_iota(jnp.int32, (tok, lanes), 0)
    t_col = lax.broadcasted_iota(jnp.int32, (tok, lanes), 1) & (tok - 1)
    eye = lax.broadcasted_iota(jnp.int32, (tok, tok), 0) == lax.broadcasted_iota(
        jnp.int32, (tok, tok), 1
    )

    def spread(values):
        grid = jnp.where(eye, jnp.broadcast_to(values, (tok, tok)), 0)
        return jnp.broadcast_to(jnp.sum(grid, axis=1, keepdims=True), (tok, lanes))

    ids = [spread(ids_ref[k : k + 1, :]) for k in range(TOP)]
    quota = [spread(quota_ref[k : k + 1, :].astype(F32)) for k in range(TOP)]
    place_of, share_of = [], []
    lane_quota = [
        jnp.sum(jnp.where(t_row == t_col, q, 0.0), axis=0, keepdims=True) for q in quota
    ]
    whole_quota = lane_quota[0] + lane_quota[1]
    for k in range(TOP):
        mine = jnp.sum(jnp.where(t_row == t_col, ids[k], 0), axis=0, keepdims=True)
        before = jnp.zeros((tok, lanes), jnp.int32)
        for other_k in range(TOP):
            before = before + jnp.where((ids[other_k] == mine) & (t_row < t_col), 1, 0)
        position = jnp.sum(before, axis=0, keepdims=True)
        ahead = ((mine // HALVES) + NX - xx) & (NX - 1)
        place_of.append((ahead * HALVES + (mine & (HALVES - 1))) * CAP + position)
        share_of.append(lane_quota[k] / whole_quota)
    s_row = lax.broadcasted_iota(jnp.int32, (slots * SPLIT, lanes), 0)
    s_col = lax.broadcasted_iota(jnp.int32, (slots * SPLIT, lanes), 1)
    same_piece = (s_row & (SPLIT - 1)) == (s_col >> (tok.bit_length() - 1))
    hits = [same_piece & ((s_row >> 3) == place_of[k]) for k in range(TOP)]
    pick = (jnp.where(hits[0], 1.0, 0.0) + jnp.where(hits[1], 1.0, 0.0)).astype(BF16)

    for c in range(2):
        stacked = jnp.concatenate(
            [
                tok_ref[:, c * half + o * piece : c * half + (o + 1) * piece]
                for o in range(SPLIT)
            ],
            axis=0,
        )
        chosen = jnp.dot(pick, stacked, preferred_element_type=F32).astype(BF16)
        packed[c] = chosen.reshape(NX, HALVES, CAP * SPLIT, piece)
        arr[c, 0, pl.ds(zz, 1)] = packed[c, 0, pl.ds(zz // GROUP, 1)]

    pl.semaphore_wait(barrier, n_ex - 1 + 3)

    def to_expert(k, c, dz):
        z_to = lax.rem(zz + dz, NZ)
        x_to = lax.rem(xx + k, NX)
        return pltpu.make_async_remote_copy(
            packed.at[c, k, z_to // GROUP], arr.at[c, k, zz],
            dsend.at[c, k, dz], drecv.at[c, k, zz],
            device_id={"expert": x_to * NZ + z_to}, device_id_type=MESH,
        )

    def expert_arrival(k, c, z_from):
        return pltpu.make_async_remote_copy(
            packed.at[c, k, 0], arr.at[c, k, z_from], dsend.at[c, k, 0], drecv.at[c, k, z_from],
            device_id={"expert": ex}, device_id_type=MESH,
        )

    def to_dp(src, dst, send, recv, peer):
        return pltpu.make_async_remote_copy(
            src, dst, send, recv, device_id={"dp": peer}, device_id_type=MESH
        )

    def g_copy(k, c, n):
        block, cols, peer = [
            (dp, both(c), up), (dp, both(c), down), (dp, both(c), other),
            (down, lo(c), up), (up, hi(c), down),
            (down, both(c), other), (up, both(c), other), (far, both(c), other),
        ][n]
        view = xall.at[k, block, :, cols]
        return to_dp(view, view, gsend.at[c, k, n], grecv.at[c, k, n], peer)

    def r_copy(k, c, n):
        send, recv = rsend.at[c, k, n], rrecv.at[c, k, n]
        if n < 4:
            place = [y_far, y_up, y_down, y][n]
            return to_dp(
                part.at[k, place * 2 + (1 - core), :, both(c)],
                fromcore.at[k, place, :, both(c)], send, recv, other,
            )
        src, cols, dst, peer = [
            (far, lo(c), ringa.at[c, k], up),
            (far, hi(c), ringb.at[c, k], down),
            (up, hi(c), lasta.at[k, :, hi(c)], up),
            (down, lo(c), lastb.at[k, :, lo(c)], down),
            (up, lo(c), lasta.at[k, :, lo(c)], up),
            (down, hi(c), lastb.at[k, :, hi(c)], down),
        ][n - 4]
        return to_dp(part.at[k, src, :, cols], dst, send, recv, peer)

    def to_owner(k, c, dz):
        z_to = lax.rem(zz + dz, NZ)
        x_to = lax.rem(xx + NX - k, NX)
        return pltpu.make_async_remote_copy(
            outgo.at[c, k, z_to], ret.at[c, k, zz], bsend.at[c, k, dz], brecv.at[c, k, zz],
            device_id={"expert": x_to * NZ + z_to}, device_id_type=MESH,
        )

    def owner_arrival(k, c, z_from):
        return pltpu.make_async_remote_copy(
            outgo.at[c, k, 0], ret.at[c, k, z_from], bsend.at[c, k, 0], brecv.at[c, k, z_from],
            device_id={"expert": ex}, device_id_type=MESH,
        )

    def each_z(k, action):
        def one(z, inner):
            action(z)
            return inner

        lax.fori_loop(0, NZ, one, 0)

    def send_all(k, carry):
        for c in range(2):
            def one(dz):
                @pl.when((k != 0) | (dz != 0))
                def _():
                    to_expert(k, c, dz).start()

            each_z(k, one)
        return carry

    lax.fori_loop(0, NCHUNK, send_all, 0)

    perm[1] = jnp.where(p_col == (p_row & (SPLIT - 1)) * rows + (p_row >> 3), 1.0, 0.0).astype(BF16)
    mix_t = jnp.where(hits[0], share_of[0], 0.0) + jnp.where(hits[1], share_of[1], 0.0)
    mix[...] = mix_t.T

    def stage_rows(k, c):
        def one(z_from):
            @pl.when((k != 0) | (z_from != zz))
            def _():
                expert_arrival(k, c, z_from).wait_recv()

        each_z(k, one)
        flat = arr[c, k].reshape(NZ * CAP * SPLIT, piece)
        sorted_rows = jnp.dot(perm[0], flat, preferred_element_type=F32).astype(BF16)
        for o in range(SPLIT):
            xall[k, dp, :, c * half + o * piece : c * half + (o + 1) * piece] = sorted_rows[
                o * rows : (o + 1) * rows
            ]
        for n in range(3):
            g_copy(k, c, n).start()

    def stage_forward(k, c):
        g_copy(k, c, 0).wait_recv()
        g_copy(k, c, 3).start()
        g_copy(k, c, 5).start()
        g_copy(k, c, 1).wait_recv()
        g_copy(k, c, 4).start()
        g_copy(k, c, 6).start()

    def stage_far(k, c):
        g_copy(k, c, 3).wait_recv()
        g_copy(k, c, 4).wait_recv()
        g_copy(k, c, 7).start()

    def stage_compute(k):
        for c in range(2):
            for n in (2, 5, 6, 7):
                g_copy(k, c, n).wait_recv()

        @pl.when(k == 0)
        def _():
            for load in loads:
                load.wait()

        for m in range(2):
            x_in = xall[k, m * NY : (m + 1) * NY].reshape(NY * rows, feature)
            gate = jnp.dot(x_in, wg[...], preferred_element_type=F32)
            up_act = jnp.dot(x_in, wu[...], preferred_element_type=F32)
            hid[m * NY * rows : (m + 1) * NY * rows] = (
                gate * (1.0 / (1.0 + jnp.exp(-gate))) * up_act
            ).astype(BF16)

        wide = half // 4
        for c in range(2):
            def down_block(n, carry):
                cols = pl.ds(pl.multiple_of(c * half + n * wide, wide), wide)
                got = jnp.dot(hid[...], wd[:, cols], preferred_element_type=F32).astype(BF16)
                part[k, :, :, cols] = got.reshape(2 * NY, rows, wide)
                return carry

            lax.fori_loop(0, 4, down_block, 0)
            for n in range(4):
                r_copy(k, c, n).start()

    def join(k, c, place):
        mine = place * 2 + core
        cols = both(c)
        total = part[k, mine, :, cols].astype(F32) + fromcore[k, place, :, cols].astype(F32)
        part[k, mine, :, cols] = total.astype(BF16)

    def stage_ring(k, c):
        r_copy(k, c, 0).wait_recv()
        join(k, c, y_far)
        r_copy(k, c, 4).start()
        r_copy(k, c, 5).start()
        r_copy(k, c, 1).wait_recv()
        join(k, c, y_up)
        r_copy(k, c, 6).start()
        r_copy(k, c, 2).wait_recv()
        join(k, c, y_down)
        r_copy(k, c, 7).start()

    def stage_last(k, c):
        r_copy(k, c, 4).wait_recv()
        part[k, up, :, lo(c)] = (
            part[k, up, :, lo(c)].astype(F32) + ringa[c, k].astype(F32)
        ).astype(BF16)
        r_copy(k, c, 8).start()
        r_copy(k, c, 5).wait_recv()
        part[k, down, :, hi(c)] = (
            part[k, down, :, hi(c)].astype(F32) + ringb[c, k].astype(F32)
        ).astype(BF16)
        r_copy(k, c, 9).start()

    def stage_back(k, c):
        r_copy(k, c, 3).wait_recv()
        for n in (6, 7, 8, 9):
            r_copy(k, c, n).wait_recv()
        pieces = []
        for o in range(SPLIT):
            cols = slice(c * half + o * piece, c * half + (o + 1) * piece)
            total = (
                part[k, dp, :, cols].astype(F32)
                + fromcore[k, y, :, cols].astype(F32)
                + lasta[k, :, cols].astype(F32)
                + lastb[k, :, cols].astype(F32)
            )
            pieces.append(total.astype(BF16))
        block = jnp.concatenate(pieces, axis=0)
        sorted_rows = jnp.dot(perm[1], block, preferred_element_type=F32).astype(BF16)
        outgo[c, k] = sorted_rows.reshape(NZ, CAP * SPLIT, piece)

        def one(dz):
            @pl.when((k != 0) | (dz != 0))
            def _():
                to_owner(k, c, dz).start()

        each_z(k, one)

        @pl.when(k == 0)
        def _():
            ret[c, 0, pl.ds(zz, 1)] = outgo[c, 0, pl.ds(zz, 1)]

    def step(i, carry):
        j = i - 1
        for stage, lag in STAGES:
            k = j - lag

            @pl.when((k >= 0) & (k < NCHUNK))
            def _(stage=stage, k=k):
                if stage == "compute":
                    stage_compute(k)
                    return
                name, c = stage.split("_")
                todo = {
                    "rows": stage_rows, "forward": stage_forward, "far": stage_far,
                    "ring": stage_ring, "last": stage_last, "back": stage_back,
                }[name]
                todo(k, int(c))

        return carry

    lax.fori_loop(0, NCHUNK + 3, step, 0)

    sums = []
    for c in range(2):
        def arrived(k, carry):
            def one(z):
                @pl.when((k != 0) | (z != zz))
                def _():
                    owner_arrival(k, c, z).wait_recv()

            each_z(k, one)
            return carry

        lax.fori_loop(0, NCHUNK, arrived, 0)
        sums = []
        for k in range(NX):
            for h in range(HALVES):
                total = ret[c, k, h * GROUP].astype(F32)
                for g in range(1, GROUP):
                    total = total + ret[c, k, h * GROUP + g].astype(F32)
                sums.append(total)
        mixed = jnp.dot(
            mix[...], jnp.concatenate(sums, axis=0),
            preferred_element_type=F32, precision=lax.Precision.HIGHEST,
        ).astype(BF16)
        for o in range(SPLIT):
            out_ref[:, c * half + o * piece : c * half + (o + 1) * piece] = mixed[
                o * tok : (o + 1) * tok
            ]

    def drain(k, carry):
        for c in range(2):
            def one(z):
                @pl.when((k != 0) | (z != 0))
                def _():
                    to_expert(k, c, z).wait_send()
                    to_owner(k, c, z).wait_send()

            each_z(k, one)
            for n in range(8):
                g_copy(k, c, n).wait_send()
            for n in range(10):
                r_copy(k, c, n).wait_send()
        return carry

    lax.fori_loop(0, NCHUNK, drain, 0)


def on_device(tokens, expert_ids, gate_quota, w_gate, w_up, w_down):
    tok_rows, feature = tokens.shape
    width = w_gate.shape[2]
    half = feature // 2
    piece = half // SPLIT
    rows = NZ * CAP
    whole = pl.BlockSpec(memory_space=pltpu.VMEM)
    anywhere = pl.BlockSpec(memory_space=pl.ANY)
    dma = pltpu.SemaphoreType.DMA
    return pl.pallas_call(
        moe_kernel,
        out_shape=jax.ShapeDtypeStruct((tok_rows, feature), BF16),
        in_specs=[anywhere] * 6,
        out_specs=whole,
        scratch_shapes=[
            pltpu.VMEM((tok_rows, feature), BF16),
            pltpu.VMEM((TOP, tok_rows), jnp.int32),
            pltpu.VMEM((TOP, tok_rows), jnp.int32),
            pltpu.VMEM((2, NX, HALVES, CAP * SPLIT, piece), BF16),
            pltpu.VMEM((2, NX, NZ, CAP * SPLIT, piece), BF16),
            pltpu.VMEM((NX, 2 * NY, rows, feature), BF16),
            pltpu.VMEM((feature, width), BF16),
            pltpu.VMEM((feature, width), BF16),
            pltpu.VMEM((width, feature), BF16),
            pltpu.VMEM((2 * NY * rows, width), BF16),
            pltpu.VMEM((NX, 2 * NY, rows, feature), BF16),
            pltpu.VMEM((NX, NY, rows, feature), BF16),
            pltpu.VMEM((2, NX, rows, feature // 4), BF16),
            pltpu.VMEM((2, NX, rows, feature // 4), BF16),
            pltpu.VMEM((NX, rows, feature), BF16),
            pltpu.VMEM((NX, rows, feature), BF16),
            pltpu.VMEM((2, NX, NZ, CAP * SPLIT, piece), BF16),
            pltpu.VMEM((2, NX, NZ, CAP * SPLIT, piece), BF16),
            pltpu.VMEM((2, rows * SPLIT, rows * SPLIT), BF16),
            pltpu.VMEM((SPLIT * tok_rows, EXPERTS * CAP * SPLIT), F32),
            dma((6,)),
            dma((2, NX, NZ)),
            dma((2, NX, NZ)),
            dma((2, NX, 8)),
            dma((2, NX, 8)),
            dma((2, NX, 10)),
            dma((2, NX, 10)),
            dma((2, NX, NZ)),
            dma((2, NX, NZ)),
        ],
        compiler_params=pltpu.CompilerParams(
            collective_id=0, has_side_effects=True, vmem_limit_bytes=64 * 1024 * 1024 - 65536
        ),
        name="moe",
    )(tokens, expert_ids.T, gate_quota.T, w_gate, w_up, w_down)


def solution(mesh):
    return jax.shard_map(
        on_device,
        mesh=mesh,
        in_specs=(
            P(("dp", "expert"), None),
            P(("dp", "expert"), None),
            P(("dp", "expert"), None),
            P("expert", None, "dp"),
            P("expert", None, "dp"),
            P("expert", "dp", None),
        ),
        out_specs=P(("dp", "expert"), None),
        check_vma=False,
    )
```

time: 324 us -> 145 us (0.45)
  waiting for transfers between devices: 195 us -> 0 us
  Pallas kernels: 0 us -> 141 us
  blocking collectives: 58.9 us -> 0 us
  matrix products: 29.5 us -> 0 us
  between operations: 13.5 us -> 0.01 us
  local copies, waits for them, and re-layouts: 12.4 us -> 1.57 us
  starting transfers between devices: 9.84 us -> 0 us
  other arithmetic: 4.86 us -> 0 us
    pallas_call x0 -> x1, Pallas kernels: none -> 141 us  [on_device(): pl.pallas_call(moe_kernel, out_shape=jax.ShapeDtypeStruct((tok_rows, feat...]
    reduce_scatter x1 -> x0, waiting for transfers between devices: 74.6 us -> none  [on_device(): lax.psum_scatter(jnp.dot(hidden, down_rows, preferred_element_type=jnp.fl...]
    all_gather x1 -> x0, waiting for transfers between devices: 71.4 us -> none  [on_device(): lax.all_gather(flat_rows, 'dp', axis=0, tiled=True)]
    all_to_all x1 -> x0, blocking collectives: 58.9 us -> none  [on_device(): lax.all_to_all(outgoing, 'expert', split_axis=0, concat_axis=0, tiled=True)]
    all_to_all x1 -> x0, waiting for transfers between devices: 48.9 us -> none  [on_device(): lax.all_to_all(summed.reshape(expert_count, CAP, feature_dim).astype(jnp....]
    dot_general x3 -> x0, matrix products: 29.5 us -> none  [the longest x1 19.4 us: on_device(): jnp.dot(hidden, down_rows, preferred_element_type=jnp.float32)]
    all_to_all x1 -> x0, starting transfers between devices: 9.8 us -> none  [on_device(): lax.all_to_all(summed.reshape(expert_count, CAP, feature_dim).astype(jnp....]
    reshape x6 -> x0, local copies, waits for them, and re-layouts: 5.61 us -> none  [the longest x1 3.65 us: on_device(): flat_rows = arrived.reshape(expert_count * CAP, feature_dim)]
  transfers between devices with their start and end apart: 3 -> 0, of which waited for: 3 -> 0; matrix products, arithmetic and copies ran while one was open for 0% -> 0% of each run, Pallas kernels for 0% -> 0%
where the time goes in v2:
time: 145 us; the launch traced here: 143 us
  Pallas kernels  141 us (97%)
  local copies, waits for them, and re-layouts  1.57 us (1%)
    pallas_call x1, Pallas kernels, on_device(): pl.pallas_call(moe_kernel, out_shape=jax.ShapeDtypeStruct((tok_rows, feat...  141 us

profile of v2, /device:TPU:1, one launch (start us, length us, event | category | flops | bytes accessed | tf_op | source)
XLA Modules:
  0.0 142.9 jit_solution(15710592045662543468)
XLA Ops:
  0.0 141.3 %moe.1 = bf16[16,4096]{1,0:T(8,128)(2,1)} custom-call(bf16[16,4096]{1,0:T(8,128)(2,1)} %tok_hbm.1, s32[2,16]{1,0:T(2,128)} %bitcast.2, s32[2,16]{1,0:T(2,128)} %bitcast.3, bf16[1,4096,256]{2,1,0:T(8,128)(2,1)} %wg_hbm.1, bf16[1,4096,256]{2,1,0:T(8,128)(2,1)} %wu_hbm.1, bf16[1,256,4096]{2,1,0:T(8,128)(2,1)} %wd_hbm.1), custom_call_target="tpu_custom_call" | custom-call | tf_op jit(solution)/shard_map/moe/pallas_call | solution.py:421
  141.3 1.6 %copy.8 = bf16[16,4096]{1,0:T(8,128)(2,1)} copy(bf16[16,4096]{1,0:T(8,128)(2,1)} %moe.1) | data formatting | bytes 262144

commit v3 on v2

--- a/solution.py
+++ b/solution.py
@@ -16,20 +16,36 @@
 GROUP = NZ // HALVES
 SPLIT = 8
 NCHUNK = NX
+WIDE_IN = 2
+WIDE_OUT = 1
 F32 = jnp.float32
 BF16 = jnp.bfloat16
 
+STEPS = 17
 STAGES = (
-    ("forward_0", 0), ("rows_0", -1), ("forward_1", 0), ("rows_1", -1),
-    ("ring_0", 1), ("ring_1", 1), ("far_0", 0), ("far_1", 0), ("compute", 0),
-    ("back_0", 2), ("back_1", 2), ("last_0", 1), ("last_1", 1),
+    ("rows_wide", (2,), (9,)),
+    ("back_1", (0, 2, 3), (10, 15, 16)),
+    ("rows_0", (0, 1, 2, 3), (0, 1, 2, 3)),
+    ("rows_1", (0, 1, 3), (0, 1, 7)),
+    ("ring_1", (0, 2, 3), (6, 11, 13)),
+    ("last_1", (0, 2, 3), (7, 13, 14)),
+    ("ring_0", (0, 1, 2, 3), (6, 8, 10, 14)),
+    ("forward_1", (0, 1, 3), (1, 4, 9)),
+    ("back_0", (0, 1, 2, 3), (10, 13, 14, 16)),
+    ("far_1", (0, 1, 3), (4, 6, 10)),
+    ("compute", (0, 1, 2, 3), (5, 7, 9, 12)),
+    ("forward_0", (0, 1, 2, 3), (0, 3, 4, 7)),
+    ("back_wide", (1,), (14,)),
+    ("last_0", (0, 1, 2, 3), (8, 11, 12, 15)),
+    ("ring_wide", (1,), (7,)),
+    ("far_0", (0, 1, 2, 3), (3, 6, 8, 9)),
 )
 
 
 def moe_kernel(
     tok_hbm, ids_hbm, quota_hbm, wg_hbm, wu_hbm, wd_hbm, out_ref,
     tok_ref, ids_ref, quota_ref, packed, arr, xall, wg, wu, wd, hid, part, fromcore, ringa, ringb, lasta, lastb, outgo, ret,
-    perm, mix, w_sem, dsend, drecv, gsend, grecv, rsend, rrecv, bsend, brecv,
+    spread, arr_wide, out_wide, ret_wide, fin, fin_in, perm, mix, w_sem, dsend, drecv, gsend, grecv, rsend, rrecv, bsend, brecv, ysend, yrecv,
 ):
     tok, feature = tok_ref.shape
     half = feature // 2
@@ -68,7 +84,7 @@
         return carry
 
     lax.fori_loop(1, n_ex, greet, 0)
-    for peer in (up, down, other):
+    for peer in (up, down, far, other):
         pl.semaphore_signal(barrier, inc=1, device_id={"dp": peer}, device_id_type=MESH)
 
     first_loads = [
@@ -100,12 +116,12 @@
         jnp.int32, (tok, tok), 1
     )
 
-    def spread(values):
+    def as_column(values):
         grid = jnp.where(eye, jnp.broadcast_to(values, (tok, tok)), 0)
         return jnp.broadcast_to(jnp.sum(grid, axis=1, keepdims=True), (tok, lanes))
 
-    ids = [spread(ids_ref[k : k + 1, :]) for k in range(TOP)]
-    quota = [spread(quota_ref[k : k + 1, :].astype(F32)) for k in range(TOP)]
+    ids = [as_column(ids_ref[k : k + 1, :]) for k in range(TOP)]
+    quota = [as_column(quota_ref[k : k + 1, :].astype(F32)) for k in range(TOP)]
     place_of, share_of = [], []
     lane_quota = [
         jnp.sum(jnp.where(t_row == t_col, q, 0.0), axis=0, keepdims=True) for q in quota
@@ -138,7 +154,9 @@
         packed[c] = chosen.reshape(NX, HALVES, CAP * SPLIT, piece)
         arr[c, 0, pl.ds(zz, 1)] = packed[c, 0, pl.ds(zz // GROUP, 1)]
 
-    pl.semaphore_wait(barrier, n_ex - 1 + 3)
+    spread[:, pl.ds(y, 1)] = packed[1, WIDE_IN][:, None]
+
+    pl.semaphore_wait(barrier, n_ex - 1 + 4)
 
     def to_expert(k, c, dz):
         z_to = lax.rem(zz + dz, NZ)
@@ -147,6 +165,51 @@
             packed.at[c, k, z_to // GROUP], arr.at[c, k, zz],
             dsend.at[c, k, dz], drecv.at[c, k, zz],
             device_id={"expert": x_to * NZ + z_to}, device_id_type=MESH,
+        )
+
+    def to_expert_wide(dz):
+        z_to = lax.rem(zz + dz, NZ)
+        x_to = lax.rem(xx + WIDE_IN, NX)
+        return pltpu.make_async_remote_copy(
+            spread.at[z_to // GROUP], arr_wide.at[zz],
+            dsend.at[1, WIDE_IN, dz], drecv.at[1, WIDE_IN, zz],
+            device_id={"expert": x_to * NZ + z_to}, device_id_type=MESH,
+        )
+
+    def expert_arrival_wide(z_from):
+        return pltpu.make_async_remote_copy(
+            spread.at[0], arr_wide.at[z_from],
+            dsend.at[1, WIDE_IN, 0], drecv.at[1, WIDE_IN, z_from],
+            device_id={"expert": ex}, device_id_type=MESH,
+        )
+
+    def along_y(d):
+        peer = lax.rem(y + d, NY) * 2 + core
+        return to_dp(
+            packed.at[1, WIDE_IN], spread.at[:, y], ysend.at[0, d - 1], yrecv.at[0, d - 1], peer
+        )
+
+    def to_owner_wide(dz):
+        z_to = lax.rem(zz + dz, NZ)
+        x_to = lax.rem(xx + NX - WIDE_OUT, NX)
+        return pltpu.make_async_remote_copy(
+            out_wide.at[z_to], ret_wide.at[zz],
+            bsend.at[1, WIDE_OUT, dz], brecv.at[1, WIDE_OUT, zz],
+            device_id={"expert": x_to * NZ + z_to}, device_id_type=MESH,
+        )
+
+    def owner_arrival_wide(z_from):
+        return pltpu.make_async_remote_copy(
+            out_wide.at[0], ret_wide.at[z_from],
+            bsend.at[1, WIDE_OUT, 0], brecv.at[1, WIDE_OUT, z_from],
+            device_id={"expert": ex}, device_id_type=MESH,
+        )
+
+    def home_y(d):
+        y_to = lax.rem(y + d, NY)
+        return to_dp(
+            fin.at[y_to], fin_in.at[d - 1], ysend.at[1, d - 1], yrecv.at[1, d - 1],
+            y_to * 2 + core,
         )
 
     def expert_arrival(k, c, z_from):
@@ -208,6 +271,9 @@
 
         lax.fori_loop(0, NZ, one, 0)
 
+    for d in range(1, NY):
+        along_y(d).start()
+
     def send_all(k, carry):
         for c in range(2):
             def one(dz):
@@ -215,7 +281,10 @@
                 def _():
                     to_expert(k, c, dz).start()
 
-            each_z(k, one)
+            if c == 0:
+                each_z(k, one)
+            else:
+                pl.when(k != WIDE_IN)(lambda: each_z(k, one))
         return carry
 
     lax.fori_loop(0, NCHUNK, send_all, 0)
@@ -223,6 +292,10 @@
     perm[1] = jnp.where(p_col == (p_row & (SPLIT - 1)) * rows + (p_row >> 3), 1.0, 0.0).astype(BF16)
     mix_t = jnp.where(hits[0], share_of[0], 0.0) + jnp.where(hits[1], share_of[1], 0.0)
     mix[...] = mix_t.T
+
+    for d in range(1, NY):
+        along_y(d).wait_recv()
+    each_z(0, lambda dz: to_expert_wide(dz).start())
 
     def stage_rows(k, c):
         def one(z_from):
@@ -239,6 +312,17 @@
             ]
         for n in range(3):
             g_copy(k, c, n).start()
+
+    def stage_rows_wide():
+        each_z(0, lambda z_from: expert_arrival_wide(z_from).wait_recv())
+        for n, place in ((2, y), (5, y_down), (6, y_up), (7, y_far)):
+            flat = arr_wide[:, pl.ds(place, 1)].reshape(NZ * CAP * SPLIT, piece)
+            sorted_rows = jnp.dot(perm[0], flat, preferred_element_type=F32).astype(BF16)
+            for o in range(SPLIT):
+                xall[WIDE_IN, place * 2 + core, :, half + o * piece : half + (o + 1) * piece] = (
+                    sorted_rows[o * rows : (o + 1) * rows]
+                )
+            g_copy(WIDE_IN, 1, n).start()
 
     def stage_forward(k, c):
         g_copy(k, c, 0).wait_recv()
@@ -301,6 +385,35 @@
         join(k, c, y_down)
         r_copy(k, c, 7).start()
 
+    def to_pieces(k, c, place, extra):
+        pieces = []
+        for o in range(SPLIT):
+            cols = slice(c * half + o * piece, c * half + (o + 1) * piece)
+            total = part[k, place * 2 + core, :, cols].astype(F32)
+            for more in [fromcore.at[k, place]] + extra:
+                total = total + more[:, cols].astype(F32)
+            pieces.append(total.astype(BF16))
+        block = jnp.concatenate(pieces, axis=0)
+        return jnp.dot(perm[1], block, preferred_element_type=F32).astype(BF16)
+
+    def stage_ring_wide():
+        for n, place in ((0, y_far), (1, y_up), (2, y_down), (3, y)):
+            r_copy(WIDE_OUT, 1, n).wait_recv()
+            sorted_rows = to_pieces(WIDE_OUT, 1, place, [])
+            out_wide[:, pl.ds(place, 1)] = sorted_rows.reshape(NZ, 1, CAP * SPLIT, piece)
+        each_z(0, lambda dz: to_owner_wide(dz).start())
+
+    def stage_back_wide():
+        each_z(0, lambda z_from: owner_arrival_wide(z_from).wait_recv())
+        for place in range(NY):
+            for h in range(HALVES):
+                total = ret_wide[h * GROUP, place].astype(F32)
+                for g in range(1, GROUP):
+                    total = total + ret_wide[h * GROUP + g, place].astype(F32)
+                fin[place, h] = total.astype(BF16)
+        for d in range(1, NY):
+            home_y(d).start()
+
     def stage_last(k, c):
         r_copy(k, c, 4).wait_recv()
         part[k, up, :, lo(c)] = (
@@ -317,18 +430,7 @@
         r_copy(k, c, 3).wait_recv()
         for n in (6, 7, 8, 9):
             r_copy(k, c, n).wait_recv()
-        pieces = []
-        for o in range(SPLIT):
-            cols = slice(c * half + o * piece, c * half + (o + 1) * piece)
-            total = (
-                part[k, dp, :, cols].astype(F32)
-                + fromcore[k, y, :, cols].astype(F32)
-                + lasta[k, :, cols].astype(F32)
-                + lastb[k, :, cols].astype(F32)
-            )
-            pieces.append(total.astype(BF16))
-        block = jnp.concatenate(pieces, axis=0)
-        sorted_rows = jnp.dot(perm[1], block, preferred_element_type=F32).astype(BF16)
+        sorted_rows = to_pieces(k, c, y, [lasta.at[k], lastb.at[k]])
         outgo[c, k] = sorted_rows.reshape(NZ, CAP * SPLIT, piece)
 
         def one(dz):
@@ -342,26 +444,40 @@
         def _():
             ret[c, 0, pl.ds(zz, 1)] = outgo[c, 0, pl.ds(zz, 1)]
 
+    todo = {
+        "rows": stage_rows, "forward": stage_forward, "far": stage_far,
+        "ring": stage_ring, "last": stage_last, "back": stage_back,
+    }
+
+    def run(stage, k):
+        name, _, c = stage.partition("_")
+        if stage == "compute":
+            stage_compute(k)
+        elif stage == "rows_wide":
+            stage_rows_wide()
+        elif stage == "ring_wide":
+            stage_ring_wide()
+        elif stage == "back_wide":
+            stage_back_wide()
+        else:
+            todo[name](k, int(c))
+
     def step(i, carry):
-        j = i - 1
-        for stage, lag in STAGES:
-            k = j - lag
-
-            @pl.when((k >= 0) & (k < NCHUNK))
+        for stage, chunks, due in STAGES:
+            k = chunks[0]
+            for n in range(1, len(due)):
+                k = k + jnp.where(i >= due[n], chunks[n] - chunks[n - 1], 0)
+            now = i == due[0]
+            for at in due[1:]:
+                now = now | (i == at)
+
+            @pl.when(now)
             def _(stage=stage, k=k):
-                if stage == "compute":
-                    stage_compute(k)
-                    return
-                name, c = stage.split("_")
-                todo = {
-                    "rows": stage_rows, "forward": stage_forward, "far": stage_far,
-                    "ring": stage_ring, "last": stage_last, "back": stage_back,
-                }[name]
-                todo(k, int(c))
+                run(stage, k)
 
         return carry
 
-    lax.fori_loop(0, NCHUNK + 3, step, 0)
+    lax.fori_loop(0, STEPS, step, 0)
 
     sums = []
     for c in range(2):
@@ -371,16 +487,27 @@
                 def _():
                     owner_arrival(k, c, z).wait_recv()
 
-            each_z(k, one)
+            if c == 0:
+                each_z(k, one)
+            else:
+                pl.when(k != WIDE_OUT)(lambda: each_z(k, one))
             return carry
 
         lax.fori_loop(0, NCHUNK, arrived, 0)
+        if c == 1:
+            for d in range(1, NY):
+                home_y(d).wait_recv()
         sums = []
         for k in range(NX):
             for h in range(HALVES):
-                total = ret[c, k, h * GROUP].astype(F32)
-                for g in range(1, GROUP):
-                    total = total + ret[c, k, h * GROUP + g].astype(F32)
+                if (c, k) == (1, WIDE_OUT):
+                    total = fin[pl.ds(y, 1), h].astype(F32).reshape(CAP * SPLIT, piece)
+                    for d in range(NY - 1):
+                        total = total + fin_in[d, h].astype(F32)
+                else:
+                    total = ret[c, k, h * GROUP].astype(F32)
+                    for g in range(1, GROUP):
+                        total = total + ret[c, k, h * GROUP + g].astype(F32)
                 sums.append(total)
         mixed = jnp.dot(
             mix[...], jnp.concatenate(sums, axis=0),
@@ -393,20 +520,48 @@
 
     def drain(k, carry):
         for c in range(2):
-            def one(z):
+            def one_in(z):
                 @pl.when((k != 0) | (z != 0))
                 def _():
                     to_expert(k, c, z).wait_send()
+
+            def one_out(z):
+                @pl.when((k != 0) | (z != 0))
+                def _():
                     to_owner(k, c, z).wait_send()
 
-            each_z(k, one)
-            for n in range(8):
+            def narrow_in():
+                each_z(k, one_in)
+                for n in (0, 1, 3, 4):
+                    g_copy(k, c, n).wait_send()
+
+            def narrow_out():
+                each_z(k, one_out)
+                for n in range(4, 10):
+                    r_copy(k, c, n).wait_send()
+
+            if c == 0:
+                narrow_in()
+                narrow_out()
+            else:
+                pl.when(k != WIDE_IN)(narrow_in)
+                pl.when(k != WIDE_OUT)(narrow_out)
+            for n in (2, 5, 6, 7):
                 g_copy(k, c, n).wait_send()
-            for n in range(10):
+            for n in range(4):
                 r_copy(k, c, n).wait_send()
         return carry
 
     lax.fori_loop(0, NCHUNK, drain, 0)
+
+    def drain_wide(dz):
+        to_expert_wide(dz).wait_send()
+        to_owner_wide(dz).wait_send()
+
+    each_z(0, drain_wide)
+    for d in range(1, NY):
+        along_y(d).wait_send()
+        home_y(d).wait_send()
 
 
 def on_device(tokens, expert_ids, gate_quota, w_gate, w_up, w_down):
@@ -442,6 +597,12 @@
             pltpu.VMEM((NX, rows, feature), BF16),
             pltpu.VMEM((2, NX, NZ, CAP * SPLIT, piece), BF16),
             pltpu.VMEM((2, NX, NZ, CAP * SPLIT, piece), BF16),
+            pltpu.VMEM((HALVES, NY, CAP * SPLIT, piece), BF16),
+            pltpu.VMEM((NZ, NY, CAP * SPLIT, piece), BF16),
+            pltpu.VMEM((NZ, NY, CAP * SPLIT, piece), BF16),
+            pltpu.VMEM((NZ, NY, CAP * SPLIT, piece), BF16),
+            pltpu.VMEM((NY, HALVES, CAP * SPLIT, piece), BF16),
+            pltpu.VMEM((NY - 1, HALVES, CAP * SPLIT, piece), BF16),
             pltpu.VMEM((2, rows * SPLIT, rows * SPLIT), BF16),
             pltpu.VMEM((SPLIT * tok_rows, EXPERTS * CAP * SPLIT), F32),
             dma((6,)),
@@ -453,6 +614,8 @@
             dma((2, NX, 10)),
             dma((2, NX, NZ)),
             dma((2, NX, NZ)),
+            dma((2, NY - 1)),
+            dma((2, NY - 1)),
         ],
         compiler_params=pltpu.CompilerParams(
             collective_id=0, has_side_effects=True, vmem_limit_bytes=64 * 1024 * 1024 - 65536

time: 145 us -> 128 us (0.88); the launches traced: 143 us -> 127 us
  Pallas kernels: 141 us -> 126 us
    pallas_call x1, Pallas kernels: 141 us -> 126 us  [on_device(): pl.pallas_call(moe_kernel, out_shape=jax.ShapeDtypeStruct((tok_rows, feat...]
where the time goes in v3:
time: 128 us; the launch traced here: 127 us
  Pallas kernels  126 us (98%)
  local copies, waits for them, and re-layouts  1.57 us (1%)
    pallas_call x1, Pallas kernels, on_device(): pl.pallas_call(moe_kernel, out_shape=jax.ShapeDtypeStruct((tok_rows, feat...  126 us

profile of v3, /device:TPU:1, one launch (start us, length us, event | category | flops | bytes accessed | tf_op | source)
XLA Modules:
  0.0 127.4 jit_solution(5382641874061716273)
XLA Ops:
  0.0 125.8 %moe.1 = bf16[16,4096]{1,0:T(8,128)(2,1)} custom-call(bf16[16,4096]{1,0:T(8,128)(2,1)} %tok_hbm.1, s32[2,16]{1,0:T(2,128)} %bitcast.2, s32[2,16]{1,0:T(2,128)} %bitcast.3, bf16[1,4096,256]{2,1,0:T(8,128)(2,1)} %wg_hbm.1, bf16[1,4096,256]{2,1,0:T(8,128)(2,1)} %wu_hbm.1, bf16[1,256,4096]{2,1,0:T(8,128)(2,1)} %wd_hbm.1), custom_call_target="tpu_custom_call" | custom-call | tf_op jit(solution)/shard_map/moe/pallas_call | solution.py:576
  125.8 1.6 %copy.8 = bf16[16,4096]{1,0:T(8,128)(2,1)} copy(bf16[16,4096]{1,0:T(8,128)(2,1)} %moe.1) | data formatting | bytes 262144

commit v4 on v3

--- a/solution.py
+++ b/solution.py
@@ -15,42 +15,96 @@
 HALVES = EXPERTS // NX
 GROUP = NZ // HALVES
 SPLIT = 8
+UNITS = (1, 1)
+NC = len(UNITS)
+WIDE = NC - 1
 NCHUNK = NX
-WIDE_IN = 2
+WIDE_IN = 1
 WIDE_OUT = 1
 F32 = jnp.float32
 BF16 = jnp.bfloat16
-
-STEPS = 17
-STAGES = (
-    ("rows_wide", (2,), (9,)),
-    ("back_1", (0, 2, 3), (10, 15, 16)),
-    ("rows_0", (0, 1, 2, 3), (0, 1, 2, 3)),
-    ("rows_1", (0, 1, 3), (0, 1, 7)),
-    ("ring_1", (0, 2, 3), (6, 11, 13)),
-    ("last_1", (0, 2, 3), (7, 13, 14)),
-    ("ring_0", (0, 1, 2, 3), (6, 8, 10, 14)),
-    ("forward_1", (0, 1, 3), (1, 4, 9)),
-    ("back_0", (0, 1, 2, 3), (10, 13, 14, 16)),
-    ("far_1", (0, 1, 3), (4, 6, 10)),
-    ("compute", (0, 1, 2, 3), (5, 7, 9, 12)),
-    ("forward_0", (0, 1, 2, 3), (0, 3, 4, 7)),
-    ("back_wide", (1,), (14,)),
-    ("last_0", (0, 1, 2, 3), (8, 11, 12, 15)),
-    ("ring_wide", (1,), (7,)),
-    ("far_0", (0, 1, 2, 3), (3, 6, 8, 9)),
+FINAL = (
+    (0, 0),
+    (0, 1),
+    (1, 0),
+    (2, 0),
+    (3, 0),
+    (1, 1),
+    (2, 1),
+    (3, 1),
 )
+
+SEGMENTS = (
+    (
+        ("rows_0", 0),
+        ("rows_1", 0),
+        ("rows_0", 1),
+        ("forward_0", 0),
+        ("rows_0", 2),
+        ("far_0", 0),
+        ("forward_1", 0),
+        ("forward_0", 1),
+        ("rows_1", 2),
+        ("far_1", 0),
+        ("forward_0", 2),
+        ("rows_0", 3),
+    ),
+    (
+        ("far_0", 1),
+        ("ring_0", 0),
+        ("rows_1", 3),
+        ("last_0", 0),
+        ("rows_wide", 1),
+        ("forward_1", 2),
+        ("far_0", 2),
+        ("ring_1", 0),
+    ),
+    (
+        ("forward_0", 3),
+        ("back_0", 0),
+        ("last_1", 0),
+        ("forward_1", 3),
+        ("ring_wide", 1),
+        ("far_1", 2),
+        ("ring_0", 1),
+    ),
+    (
+        ("back_1", 0),
+        ("far_0", 3),
+        ("ring_0", 2),
+        ("far_1", 3),
+        ("last_0", 1),
+    ),
+    (
+        ("last_0", 2),
+        ("ring_0", 3),
+        ("ring_1", 2),
+        ("back_0", 1),
+        ("last_0", 3),
+        ("last_1", 2),
+        ("back_0", 2),
+        ("ring_1", 3),
+        ("back_0", 3),
+        ("back_wide", 1),
+        ("back_1", 2),
+        ("last_1", 3),
+        ("back_1", 3),
+    ),
+)
+
+
+def unit_columns(feature):
+    wid = [feature * u // sum(UNITS) for u in UNITS]
+    return wid, [sum(wid[:c]) for c in range(NC)]
 
 
 def moe_kernel(
     tok_hbm, ids_hbm, quota_hbm, wg_hbm, wu_hbm, wd_hbm, out_ref,
     tok_ref, ids_ref, quota_ref, packed, arr, xall, wg, wu, wd, hid, part, fromcore, ringa, ringb, lasta, lastb, outgo, ret,
-    spread, arr_wide, out_wide, ret_wide, fin, fin_in, perm, mix, w_sem, dsend, drecv, gsend, grecv, rsend, rrecv, bsend, brecv, ysend, yrecv,
+    spread, arr_wide, out_wide, ret_wide, fin, fin_in, perm, mix, acc, w_sem, dsend, drecv, gsend, grecv, rsend, rrecv, bsend, brecv, ysend, yrecv,
 ):
     tok, feature = tok_ref.shape
-    half = feature // 2
-    quarter = feature // 4
-    piece = half // SPLIT
+    wid, off = unit_columns(feature)
     rows = NZ * CAP
     slots = EXPERTS * CAP
     dp = lax.axis_index("dp")
@@ -67,13 +121,17 @@
     other = y * 2 + (1 - core)
 
     def both(c):
-        return pl.ds(c * half, half)
+        return pl.ds(off[c], wid[c])
 
     def lo(c):
-        return pl.ds(c * half, quarter)
+        return pl.ds(off[c], wid[c] // 2)
 
     def hi(c):
-        return pl.ds(c * half + quarter, quarter)
+        return pl.ds(off[c] + wid[c] // 2, wid[c] // 2)
+
+    def piece_cols(c, o):
+        piece = wid[c] // SPLIT
+        return slice(off[c] + o * piece, off[c] + (o + 1) * piece)
 
     barrier = pltpu.get_barrier_semaphore()
 
@@ -142,19 +200,13 @@
     hits = [same_piece & ((s_row >> 3) == place_of[k]) for k in range(TOP)]
     pick = (jnp.where(hits[0], 1.0, 0.0) + jnp.where(hits[1], 1.0, 0.0)).astype(BF16)
 
-    for c in range(2):
-        stacked = jnp.concatenate(
-            [
-                tok_ref[:, c * half + o * piece : c * half + (o + 1) * piece]
-                for o in range(SPLIT)
-            ],
-            axis=0,
-        )
+    for c in range(NC):
+        stacked = jnp.concatenate([tok_ref[:, piece_cols(c, o)] for o in range(SPLIT)], axis=0)
         chosen = jnp.dot(pick, stacked, preferred_element_type=F32).astype(BF16)
-        packed[c] = chosen.reshape(NX, HALVES, CAP * SPLIT, piece)
-        arr[c, 0, pl.ds(zz, 1)] = packed[c, 0, pl.ds(zz // GROUP, 1)]
-
-    spread[:, pl.ds(y, 1)] = packed[1, WIDE_IN][:, None]
+        packed[c][...] = chosen.reshape(packed[c].shape)
+        arr[c][0, pl.ds(zz, 1)] = packed[c][0, pl.ds(zz // GROUP, 1)]
+
+    spread[:, pl.ds(y, 1)] = packed[WIDE][WIDE_IN][:, None]
 
     pl.semaphore_wait(barrier, n_ex - 1 + 4)
 
@@ -162,7 +214,7 @@
         z_to = lax.rem(zz + dz, NZ)
         x_to = lax.rem(xx + k, NX)
         return pltpu.make_async_remote_copy(
-            packed.at[c, k, z_to // GROUP], arr.at[c, k, zz],
+            packed[c].at[k, z_to // GROUP], arr[c].at[k, zz],
             dsend.at[c, k, dz], drecv.at[c, k, zz],
             device_id={"expert": x_to * NZ + z_to}, device_id_type=MESH,
         )
@@ -172,21 +224,21 @@
         x_to = lax.rem(xx + WIDE_IN, NX)
         return pltpu.make_async_remote_copy(
             spread.at[z_to // GROUP], arr_wide.at[zz],
-            dsend.at[1, WIDE_IN, dz], drecv.at[1, WIDE_IN, zz],
+            dsend.at[WIDE, WIDE_IN, dz], drecv.at[WIDE, WIDE_IN, zz],
             device_id={"expert": x_to * NZ + z_to}, device_id_type=MESH,
         )
 
     def expert_arrival_wide(z_from):
         return pltpu.make_async_remote_copy(
             spread.at[0], arr_wide.at[z_from],
-            dsend.at[1, WIDE_IN, 0], drecv.at[1, WIDE_IN, z_from],
+            dsend.at[WIDE, WIDE_IN, 0], drecv.at[WIDE, WIDE_IN, z_from],
             device_id={"expert": ex}, device_id_type=MESH,
         )
 
     def along_y(d):
         peer = lax.rem(y + d, NY) * 2 + core
         return to_dp(
-            packed.at[1, WIDE_IN], spread.at[:, y], ysend.at[0, d - 1], yrecv.at[0, d - 1], peer
+            packed[WIDE].at[WIDE_IN], spread.at[:, y], ysend.at[0, d - 1], yrecv.at[0, d - 1], peer
         )
 
     def to_owner_wide(dz):
@@ -194,14 +246,14 @@
         x_to = lax.rem(xx + NX - WIDE_OUT, NX)
         return pltpu.make_async_remote_copy(
             out_wide.at[z_to], ret_wide.at[zz],
-            bsend.at[1, WIDE_OUT, dz], brecv.at[1, WIDE_OUT, zz],
+            bsend.at[WIDE, WIDE_OUT, dz], brecv.at[WIDE, WIDE_OUT, zz],
             device_id={"expert": x_to * NZ + z_to}, device_id_type=MESH,
         )
 
     def owner_arrival_wide(z_from):
         return pltpu.make_async_remote_copy(
             out_wide.at[0], ret_wide.at[z_from],
-            bsend.at[1, WIDE_OUT, 0], brecv.at[1, WIDE_OUT, z_from],
+            bsend.at[WIDE, WIDE_OUT, 0], brecv.at[WIDE, WIDE_OUT, z_from],
             device_id={"expert": ex}, device_id_type=MESH,
         )
 
@@ -214,7 +266,7 @@
 
     def expert_arrival(k, c, z_from):
         return pltpu.make_async_remote_copy(
-            packed.at[c, k, 0], arr.at[c, k, z_from], dsend.at[c, k, 0], drecv.at[c, k, z_from],
+            packed[c].at[k, 0], arr[c].at[k, z_from], dsend.at[c, k, 0], drecv.at[c, k, z_from],
             device_id={"expert": ex}, device_id_type=MESH,
         )
 
@@ -241,8 +293,8 @@
                 fromcore.at[k, place, :, both(c)], send, recv, other,
             )
         src, cols, dst, peer = [
-            (far, lo(c), ringa.at[c, k], up),
-            (far, hi(c), ringb.at[c, k], down),
+            (far, lo(c), ringa[c].at[k], up),
+            (far, hi(c), ringb[c].at[k], down),
             (up, hi(c), lasta.at[k, :, hi(c)], up),
             (down, lo(c), lastb.at[k, :, lo(c)], down),
             (up, lo(c), lasta.at[k, :, lo(c)], up),
@@ -254,13 +306,13 @@
         z_to = lax.rem(zz + dz, NZ)
         x_to = lax.rem(xx + NX - k, NX)
         return pltpu.make_async_remote_copy(
-            outgo.at[c, k, z_to], ret.at[c, k, zz], bsend.at[c, k, dz], brecv.at[c, k, zz],
+            outgo[c].at[k, z_to], ret[c].at[k, zz], bsend.at[c, k, dz], brecv.at[c, k, zz],
             device_id={"expert": x_to * NZ + z_to}, device_id_type=MESH,
         )
 
     def owner_arrival(k, c, z_from):
         return pltpu.make_async_remote_copy(
-            outgo.at[c, k, 0], ret.at[c, k, z_from], bsend.at[c, k, 0], brecv.at[c, k, z_from],
+            outgo[c].at[k, 0], ret[c].at[k, z_from], bsend.at[c, k, 0], brecv.at[c, k, z_from],
             device_id={"expert": ex}, device_id_type=MESH,
         )
 
@@ -275,13 +327,13 @@
         along_y(d).start()
 
     def send_all(k, carry):
-        for c in range(2):
+        for c in range(NC):
             def one(dz):
                 @pl.when((k != 0) | (dz != 0))
                 def _():
                     to_expert(k, c, dz).start()
 
-            if c == 0:
+            if c != WIDE:
                 each_z(k, one)
             else:
                 pl.when(k != WIDE_IN)(lambda: each_z(k, one))
@@ -291,7 +343,9 @@
 
     perm[1] = jnp.where(p_col == (p_row & (SPLIT - 1)) * rows + (p_row >> 3), 1.0, 0.0).astype(BF16)
     mix_t = jnp.where(hits[0], share_of[0], 0.0) + jnp.where(hits[1], share_of[1], 0.0)
-    mix[...] = mix_t.T
+    share = mix_t.shape[0] // NX
+    for k in range(NX):
+        mix[k] = mix_t[k * share : (k + 1) * share].T
 
     for d in range(1, NY):
         along_y(d).wait_recv()
@@ -304,25 +358,23 @@
                 expert_arrival(k, c, z_from).wait_recv()
 
         each_z(k, one)
-        flat = arr[c, k].reshape(NZ * CAP * SPLIT, piece)
+        flat = arr[c][k].reshape(NZ * CAP * SPLIT, wid[c] // SPLIT)
         sorted_rows = jnp.dot(perm[0], flat, preferred_element_type=F32).astype(BF16)
         for o in range(SPLIT):
-            xall[k, dp, :, c * half + o * piece : c * half + (o + 1) * piece] = sorted_rows[
-                o * rows : (o + 1) * rows
-            ]
+            xall[k, dp, :, piece_cols(c, o)] = sorted_rows[o * rows : (o + 1) * rows]
         for n in range(3):
             g_copy(k, c, n).start()
 
     def stage_rows_wide():
         each_z(0, lambda z_from: expert_arrival_wide(z_from).wait_recv())
         for n, place in ((2, y), (5, y_down), (6, y_up), (7, y_far)):
-            flat = arr_wide[:, pl.ds(place, 1)].reshape(NZ * CAP * SPLIT, piece)
+            flat = arr_wide[:, pl.ds(place, 1)].reshape(NZ * CAP * SPLIT, wid[WIDE] // SPLIT)
             sorted_rows = jnp.dot(perm[0], flat, preferred_element_type=F32).astype(BF16)
             for o in range(SPLIT):
-                xall[WIDE_IN, place * 2 + core, :, half + o * piece : half + (o + 1) * piece] = (
-                    sorted_rows[o * rows : (o + 1) * rows]
-                )
-            g_copy(WIDE_IN, 1, n).start()
+                xall[WIDE_IN, place * 2 + core, :, piece_cols(WIDE, o)] = sorted_rows[
+                    o * rows : (o + 1) * rows
+                ]
+            g_copy(WIDE_IN, WIDE, n).start()
 
     def stage_forward(k, c):
         g_copy(k, c, 0).wait_recv()
@@ -338,7 +390,7 @@
         g_copy(k, c, 7).start()
 
     def stage_compute(k):
-        for c in range(2):
+        for c in range(NC):
             for n in (2, 5, 6, 7):
                 g_copy(k, c, n).wait_recv()
 
@@ -355,15 +407,15 @@
                 gate * (1.0 / (1.0 + jnp.exp(-gate))) * up_act
             ).astype(BF16)
 
-        wide = half // 4
-        for c in range(2):
+        wide = min(wid) // 2
+        for c in range(NC):
             def down_block(n, carry):
-                cols = pl.ds(pl.multiple_of(c * half + n * wide, wide), wide)
+                cols = pl.ds(pl.multiple_of(off[c] + n * wide, wide), wide)
                 got = jnp.dot(hid[...], wd[:, cols], preferred_element_type=F32).astype(BF16)
                 part[k, :, :, cols] = got.reshape(2 * NY, rows, wide)
                 return carry
 
-            lax.fori_loop(0, 4, down_block, 0)
+            lax.fori_loop(0, wid[c] // wide, down_block, 0)
             for n in range(4):
                 r_copy(k, c, n).start()
 
@@ -388,7 +440,7 @@
     def to_pieces(k, c, place, extra):
         pieces = []
         for o in range(SPLIT):
-            cols = slice(c * half + o * piece, c * half + (o + 1) * piece)
+            cols = piece_cols(c, o)
             total = part[k, place * 2 + core, :, cols].astype(F32)
             for more in [fromcore.at[k, place]] + extra:
                 total = total + more[:, cols].astype(F32)
@@ -398,9 +450,11 @@
 
     def stage_ring_wide():
         for n, place in ((0, y_far), (1, y_up), (2, y_down), (3, y)):
-            r_copy(WIDE_OUT, 1, n).wait_recv()
-            sorted_rows = to_pieces(WIDE_OUT, 1, place, [])
-            out_wide[:, pl.ds(place, 1)] = sorted_rows.reshape(NZ, 1, CAP * SPLIT, piece)
+            r_copy(WIDE_OUT, WIDE, n).wait_recv()
+            sorted_rows = to_pieces(WIDE_OUT, WIDE, place, [])
+            out_wide[:, pl.ds(place, 1)] = sorted_rows.reshape(
+                NZ, 1, CAP * SPLIT, wid[WIDE] // SPLIT
+            )
         each_z(0, lambda dz: to_owner_wide(dz).start())
 
     def stage_back_wide():
@@ -417,12 +471,12 @@
     def stage_last(k, c):
         r_copy(k, c, 4).wait_recv()
         part[k, up, :, lo(c)] = (
-            part[k, up, :, lo(c)].astype(F32) + ringa[c, k].astype(F32)
+            part[k, up, :, lo(c)].astype(F32) + ringa[c][k].astype(F32)
         ).astype(BF16)
         r_copy(k, c, 8).start()
         r_copy(k, c, 5).wait_recv()
         part[k, down, :, hi(c)] = (
-            part[k, down, :, hi(c)].astype(F32) + ringb[c, k].astype(F32)
+            part[k, down, :, hi(c)].astype(F32) + ringb[c][k].astype(F32)
         ).astype(BF16)
         r_copy(k, c, 9).start()
 
@@ -431,7 +485,7 @@
         for n in (6, 7, 8, 9):
             r_copy(k, c, n).wait_recv()
         sorted_rows = to_pieces(k, c, y, [lasta.at[k], lastb.at[k]])
-        outgo[c, k] = sorted_rows.reshape(NZ, CAP * SPLIT, piece)
+        outgo[c][k] = sorted_rows.reshape(NZ, CAP * SPLIT, wid[c] // SPLIT)
 
         def one(dz):
             @pl.when((k != 0) | (dz != 0))
@@ -442,7 +496,7 @@
 
         @pl.when(k == 0)
         def _():
-            ret[c, 0, pl.ds(zz, 1)] = outgo[c, 0, pl.ds(zz, 1)]
+            ret[c][0, pl.ds(zz, 1)] = outgo[c][0, pl.ds(zz, 1)]
 
     todo = {
         "rows": stage_rows, "forward": stage_forward, "far": stage_far,
@@ -451,9 +505,7 @@
 
     def run(stage, k):
         name, _, c = stage.partition("_")
-        if stage == "compute":
-            stage_compute(k)
-        elif stage == "rows_wide":
+        if stage == "rows_wide":
             stage_rows_wide()
         elif stage == "ring_wide":
             stage_ring_wide()
@@ -463,63 +515,59 @@
             todo[name](k, int(c))
 
     def step(i, carry):
-        for stage, chunks, due in STAGES:
-            k = chunks[0]
-            for n in range(1, len(due)):
-                k = k + jnp.where(i >= due[n], chunks[n] - chunks[n - 1], 0)
-            now = i == due[0]
-            for at in due[1:]:
-                now = now | (i == at)
-
-            @pl.when(now)
-            def _(stage=stage, k=k):
-                run(stage, k)
+        for at, segment in enumerate(SEGMENTS):
+            @pl.when(i == at)
+            def _(segment=segment):
+                for stage, k in segment:
+                    run(stage, k)
+
+        @pl.when(i < NCHUNK)
+        def _():
+            stage_compute(i)
 
         return carry
 
-    lax.fori_loop(0, STEPS, step, 0)
-
-    sums = []
-    for c in range(2):
-        def arrived(k, carry):
-            def one(z):
-                @pl.when((k != 0) | (z != zz))
-                def _():
-                    owner_arrival(k, c, z).wait_recv()
-
-            if c == 0:
-                each_z(k, one)
-            else:
-                pl.when(k != WIDE_OUT)(lambda: each_z(k, one))
-            return carry
-
-        lax.fori_loop(0, NCHUNK, arrived, 0)
-        if c == 1:
+    lax.fori_loop(0, NCHUNK + 1, step, 0)
+
+    for at, (k, c) in enumerate(FINAL):
+        if (c, k) == (WIDE, WIDE_OUT):
             for d in range(1, NY):
                 home_y(d).wait_recv()
+        else:
+            def one(z):
+                if k == 0:
+                    pl.when(z != zz)(lambda: owner_arrival(k, c, z).wait_recv())
+                else:
+                    owner_arrival(k, c, z).wait_recv()
+
+            each_z(k, one)
         sums = []
-        for k in range(NX):
-            for h in range(HALVES):
-                if (c, k) == (1, WIDE_OUT):
-                    total = fin[pl.ds(y, 1), h].astype(F32).reshape(CAP * SPLIT, piece)
-                    for d in range(NY - 1):
-                        total = total + fin_in[d, h].astype(F32)
-                else:
-                    total = ret[c, k, h * GROUP].astype(F32)
-                    for g in range(1, GROUP):
-                        total = total + ret[c, k, h * GROUP + g].astype(F32)
-                sums.append(total)
+        for h in range(HALVES):
+            if (c, k) == (WIDE, WIDE_OUT):
+                total = fin[pl.ds(y, 1), h].astype(F32).reshape(fin.shape[2:])
+                for d in range(NY - 1):
+                    total = total + fin_in[d, h].astype(F32)
+            else:
+                total = ret[c][k, h * GROUP].astype(F32)
+                for g in range(1, GROUP):
+                    total = total + ret[c][k, h * GROUP + g].astype(F32)
+            sums.append(total)
         mixed = jnp.dot(
-            mix[...], jnp.concatenate(sums, axis=0),
+            mix[k], jnp.concatenate(sums, axis=0),
             preferred_element_type=F32, precision=lax.Precision.HIGHEST,
-        ).astype(BF16)
-        for o in range(SPLIT):
-            out_ref[:, c * half + o * piece : c * half + (o + 1) * piece] = mixed[
-                o * tok : (o + 1) * tok
-            ]
+        )
+        seen = [kk for kk, cc in FINAL[:at] if cc == c]
+        if seen:
+            mixed = mixed + acc[c][...]
+        if len(seen) < NCHUNK - 1:
+            acc[c][...] = mixed
+        else:
+            mixed = mixed.astype(BF16)
+            for o in range(SPLIT):
+                out_ref[:, piece_cols(c, o)] = mixed[o * tok : (o + 1) * tok]
 
     def drain(k, carry):
-        for c in range(2):
+        for c in range(NC):
             def one_in(z):
                 @pl.when((k != 0) | (z != 0))
                 def _():
@@ -540,7 +588,7 @@
                 for n in range(4, 10):
                     r_copy(k, c, n).wait_send()
 
-            if c == 0:
+            if c != WIDE:
                 narrow_in()
                 narrow_out()
             else:
@@ -567,9 +615,13 @@
 def on_device(tokens, expert_ids, gate_quota, w_gate, w_up, w_down):
     tok_rows, feature = tokens.shape
     width = w_gate.shape[2]
-    half = feature // 2
-    piece = half // SPLIT
+    wid, _ = unit_columns(feature)
     rows = NZ * CAP
+    wide_piece = wid[WIDE] // SPLIT
+
+    def per_unit(shape, divisor):
+        return [pltpu.VMEM((*shape, w // divisor), BF16) for w in wid]
+
     whole = pl.BlockSpec(memory_space=pltpu.VMEM)
     anywhere = pl.BlockSpec(memory_space=pl.ANY)
     dma = pltpu.SemaphoreType.DMA
@@ -582,8 +634,8 @@
             pltpu.VMEM((tok_rows, feature), BF16),
             pltpu.VMEM((TOP, tok_rows), jnp.int32),
             pltpu.VMEM((TOP, tok_rows), jnp.int32),
-            pltpu.VMEM((2, NX, HALVES, CAP * SPLIT, piece), BF16),
-            pltpu.VMEM((2, NX, NZ, CAP * SPLIT, piece), BF16),
+            per_unit((NX, HALVES, CAP * SPLIT), SPLIT),
+            per_unit((NX, NZ, CAP * SPLIT), SPLIT),
             pltpu.VMEM((NX, 2 * NY, rows, feature), BF16),
             pltpu.VMEM((feature, width), BF16),
             pltpu.VMEM((feature, width), BF16),
@@ -591,29 +643,30 @@
             pltpu.VMEM((2 * NY * rows, width), BF16),
             pltpu.VMEM((NX, 2 * NY, rows, feature), BF16),
             pltpu.VMEM((NX, NY, rows, feature), BF16),
-            pltpu.VMEM((2, NX, rows, feature // 4), BF16),
-            pltpu.VMEM((2, NX, rows, feature // 4), BF16),
+            per_unit((NX, rows), 2),
+            per_unit((NX, rows), 2),
             pltpu.VMEM((NX, rows, feature), BF16),
             pltpu.VMEM((NX, rows, feature), BF16),
-            pltpu.VMEM((2, NX, NZ, CAP * SPLIT, piece), BF16),
-            pltpu.VMEM((2, NX, NZ, CAP * SPLIT, piece), BF16),
-            pltpu.VMEM((HALVES, NY, CAP * SPLIT, piece), BF16),
-            pltpu.VMEM((NZ, NY, CAP * SPLIT, piece), BF16),
-            pltpu.VMEM((NZ, NY, CAP * SPLIT, piece), BF16),
-            pltpu.VMEM((NZ, NY, CAP * SPLIT, piece), BF16),
-            pltpu.VMEM((NY, HALVES, CAP * SPLIT, piece), BF16),
-            pltpu.VMEM((NY - 1, HALVES, CAP * SPLIT, piece), BF16),
+            per_unit((NX, NZ, CAP * SPLIT), SPLIT),
+            per_unit((NX, NZ, CAP * SPLIT), SPLIT),
+            pltpu.VMEM((HALVES, NY, CAP * SPLIT, wide_piece), BF16),
+            pltpu.VMEM((NZ, NY, CAP * SPLIT, wide_piece), BF16),
+            pltpu.VMEM((NZ, NY, CAP * SPLIT, wide_piece), BF16),
+            pltpu.VMEM((NZ, NY, CAP * SPLIT, wide_piece), BF16),
+            pltpu.VMEM((NY, HALVES, CAP * SPLIT, wide_piece), BF16),
+            pltpu.VMEM((NY - 1, HALVES, CAP * SPLIT, wide_piece), BF16),
             pltpu.VMEM((2, rows * SPLIT, rows * SPLIT), BF16),
-            pltpu.VMEM((SPLIT * tok_rows, EXPERTS * CAP * SPLIT), F32),
+            pltpu.VMEM((NX, SPLIT * tok_rows, HALVES * CAP * SPLIT), F32),
+            [pltpu.VMEM((SPLIT * tok_rows, w // SPLIT), F32) for w in wid],
             dma((6,)),
-            dma((2, NX, NZ)),
-            dma((2, NX, NZ)),
-            dma((2, NX, 8)),
-            dma((2, NX, 8)),
-            dma((2, NX, 10)),
-            dma((2, NX, 10)),
-            dma((2, NX, NZ)),
-            dma((2, NX, NZ)),
+            dma((NC, NX, NZ)),
+            dma((NC, NX, NZ)),
+            dma((NC, NX, 8)),
+            dma((NC, NX, 8)),
+            dma((NC, NX, 10)),
+            dma((NC, NX, 10)),
+            dma((NC, NX, NZ)),
+            dma((NC, NX, NZ)),
             dma((2, NY - 1)),
             dma((2, NY - 1)),
         ],

time: 128 us -> 127 us (level)
  Pallas kernels: 126 us -> 124 us
    pallas_call x1, Pallas kernels: 126 us -> 124 us  [on_device(): pl.pallas_call(moe_kernel, out_shape=jax.ShapeDtypeStruct((tok_rows, feat...]
where the time goes in v4:
time: 127 us; the launch traced here: 126 us
  Pallas kernels  124 us (98%)
  local copies, waits for them, and re-layouts  1.57 us (1%)
    pallas_call x1, Pallas kernels, on_device(): pl.pallas_call(moe_kernel, out_shape=jax.ShapeDtypeStruct((tok_rows, feat...  124 us

profile of v4, /device:TPU:1, one launch (start us, length us, event | category | flops | bytes accessed | tf_op | source)
XLA Modules:
  0.0 125.7 jit_solution(5419717608222697764)
XLA Ops:
  0.0 124.1 %moe.1 = bf16[16,4096]{1,0:T(8,128)(2,1)} custom-call(bf16[16,4096]{1,0:T(8,128)(2,1)} %tok_hbm.1, s32[2,16]{1,0:T(2,128)} %bitcast.2, s32[2,16]{1,0:T(2,128)} %bitcast.3, bf16[1,4096,256]{2,1,0:T(8,128)(2,1)} %wg_hbm.1, bf16[1,4096,256]{2,1,0:T(8,128)(2,1)} %wu_hbm.1, bf16[1,256,4096]{2,1,0:T(8,128)(2,1)} %wd_hbm.1), custom_call_target="tpu_custom_call" | custom-call | tf_op jit(solution)/shard_map/moe/pallas_call | solution.py:628
  124.1 1.6 %copy.8 = bf16[16,4096]{1,0:T(8,128)(2,1)} copy(bf16[16,4096]{1,0:T(8,128)(2,1)} %moe.1) | data formatting | bytes 262144

commit v5 on v4

--- a/solution.py
+++ b/solution.py
@@ -339,7 +339,11 @@
                 pl.when(k != WIDE_IN)(lambda: each_z(k, one))
         return carry
 
-    lax.fori_loop(0, NCHUNK, send_all, 0)
+    lax.fori_loop(0, WIDE_IN + 1, send_all, 0)
+    for d in range(1, NY):
+        along_y(d).wait_recv()
+    each_z(0, lambda dz: to_expert_wide(dz).start())
+    lax.fori_loop(WIDE_IN + 1, NCHUNK, send_all, 0)
 
     perm[1] = jnp.where(p_col == (p_row & (SPLIT - 1)) * rows + (p_row >> 3), 1.0, 0.0).astype(BF16)
     mix_t = jnp.where(hits[0], share_of[0], 0.0) + jnp.where(hits[1], share_of[1], 0.0)
@@ -347,9 +351,6 @@
     for k in range(NX):
         mix[k] = mix_t[k * share : (k + 1) * share].T
 
-    for d in range(1, NY):
-        along_y(d).wait_recv()
-    each_z(0, lambda dz: to_expert_wide(dz).start())
 
     def stage_rows(k, c):
         def one(z_from):

time: 127 us -> 143 us (1.13)
  Pallas kernels: 124 us -> 140 us
    pallas_call x1, Pallas kernels: 124 us -> 140 us  [on_device(): pl.pallas_call(moe_kernel, out_shape=jax.ShapeDtypeStruct((tok_rows, feat...]
where the time goes in v5:
time: 143 us; the launch traced here: 141 us
  Pallas kernels  140 us (98%)
  local copies, waits for them, and re-layouts  1.57 us (1%)
    pallas_call x1, Pallas kernels, on_device(): pl.pallas_call(moe_kernel, out_shape=jax.ShapeDtypeStruct((tok_rows, feat...  140 us

profile of v5, /device:TPU:1, one launch (start us, length us, event | category | flops | bytes accessed | tf_op | source)
XLA Modules:
  0.0 141.5 jit_solution(2646374007813359695)
XLA Ops:
  0.0 139.9 %moe.1 = bf16[16,4096]{1,0:T(8,128)(2,1)} custom-call(bf16[16,4096]{1,0:T(8,128)(2,1)} %tok_hbm.1, s32[2,16]{1,0:T(2,128)} %bitcast.2, s32[2,16]{1,0:T(2,128)} %bitcast.3, bf16[1,4096,256]{2,1,0:T(8,128)(2,1)} %wg_hbm.1, bf16[1,4096,256]{2,1,0:T(8,128)(2,1)} %wu_hbm.1, bf16[1,256,4096]{2,1,0:T(8,128)(2,1)} %wd_hbm.1), custom_call_target="tpu_custom_call" | custom-call | tf_op jit(solution)/shard_map/moe/pallas_call | solution.py:629
  139.9 1.6 %copy.8 = bf16[16,4096]{1,0:T(8,128)(2,1)} copy(bf16[16,4096]{1,0:T(8,128)(2,1)} %moe.1) | data formatting | bytes 262144
